TPU v7x, 256 devices: a whole 4x4x8 slice. The times are simulated.
256 devices in a mesh: orb: 16 (over z, x_hi), cell: 16 (over y, x_lo, core).
Axes of the slice: x: 4 (x_hi: 2, x_lo: 2; x = x_hi * 2 + x_lo), y: 4, z: 8, core: 2. Of those that a mesh axis runs over, the one named last changes fastest.
Arguments:
- potentials: bfloat16 [192, 65536], P(None, 'cell'), may hold values from -6 to 6
- orbitals: bfloat16 [512, 65536], P('orb', 'cell'), may hold values from -6 to 6
- levels: float32 [512], replicated, may hold values from 0.2 to 4
- occ_index: int32 [128], replicated, may hold values from 0 to 511, as said below
- coul_rows: float32 [256, 256], replicated, may hold values from -0.375 to 0.375
- coul_cols: float32 [256, 256], replicated, may hold values from -0.375 to 0.375
Outputs:
- screened: float32 [192, 256, 256], P('orb', 'cell')
Inputs may be any that keep to these rules, and one draw needn't show every extreme that they name: `occ_index`: 128 distinct orbital numbers.
All inputs are finite; a program needn't handle non-finite values.
Results may differ from a plain program's by a relative error of at most 0.004.
Values may be sent and summed in bfloat16 or wider, within the bound.
No kernel may reach another device: no remote copies, remote signals or barrier semaphores. Data moves between devices by JAX's collectives and lax.ppermute only.
A program may use at most 64 MiB of HBM per device.

v0:
```python
import functools

import jax
import jax.numpy as jnp
from jax import lax
from jax.experimental import pallas as pl
from jax.experimental.pallas import tpu as pltpu
from jax.sharding import Mesh
from jax.sharding import PartitionSpec as P

SIDE = 256
Z, XH, Y, XL, CORE = "z", "x_hi", "y", "x_lo", "core"
CELL = (Y, XL, CORE)
ORB = (Z, XH)
CHIP = (Y, XL)
F32, BF16 = jnp.float32, jnp.bfloat16
HIGH = lax.Precision.HIGHEST
SWAP = ((0, 1), (1, 0))
WHOLE = pl.BlockSpec(memory_space=pltpu.VMEM)
ROOM = pltpu.CompilerParams(vmem_limit_bytes=20 * 2**20)


def swapped(shard, axis):
    return lax.ppermute(shard, axis, SWAP)


def exchanged(parts, axes):
    return lax.all_to_all(parts, axes, split_axis=0, concat_axis=0, tiled=True)


def split_kernel(rows_ref, out_ref):
    width = out_ref.shape[2]
    for k in range(out_ref.shape[0]):
        out_ref[k] = rows_ref[:, k * width : (k + 1) * width]


def pick_kernel(wanted_ref, rows_ref, out_ref):
    count, stored = wanted_ref.shape[0], rows_ref.shape[0]
    label = lax.broadcasted_iota(jnp.int32, (count, stored), 1)
    chosen = jnp.where(wanted_ref[...] == label, 1.0, 0.0).astype(BF16)
    picked = jnp.dot(chosen, rows_ref[...], preferred_element_type=F32).astype(BF16)
    slots = out_ref.shape[1]
    for k in range(out_ref.shape[0]):
        n = k % (count // slots)
        out_ref[k] = picked[n * slots : (n + 1) * slots]


def order_kernel(source_ref, rows_ref, out_ref):
    count = source_ref.shape[0]
    label = lax.broadcasted_iota(jnp.int32, (count, count), 1)
    order = jnp.where(source_ref[...] == label, 1.0, 0.0).astype(BF16)
    out_ref[...] = jnp.dot(order, rows_ref[...], preferred_element_type=F32).astype(BF16)


def join_kernel(near_ref, far_ref, out_ref):
    out_ref[...] = (near_ref[...] + far_ref[...]).astype(out_ref.dtype)


def products(occ, places, parts):
    return jnp.concatenate([occ[n : n + 1, :] * part for n in places for part in parts], axis=0)


def stack_kernel(first_ref, second_ref, *out_refs):
    rows = first_ref.shape[0]
    for ref in out_refs:
        ref[:rows] = first_ref[...]
        ref[rows:] = second_ref[...]


def halves(basis_ref, cut):
    rows = basis_ref.shape[0] // 2
    return basis_ref[:rows, cut], basis_ref[rows:, cut]


def project_kernel(occ_ref, basis_ref, pot_ref, out_ref, *, start, group):
    blocks, _, width = occ_ref.shape
    count, _, lanes = out_ref.shape
    per_step = 16
    outs = per_step // group

    def step(t, carry):
        places = pl.ds(pl.multiple_of(start + t * per_step, per_step), per_step)
        total = None
        for k in range(blocks):
            cut = slice(k * width, (k + 1) * width)
            parts = halves(basis_ref, cut)
            pairs = products(occ_ref[k, places, :], range(per_step), parts)
            term = lax.dot_general(
                pairs, pot_ref[:, cut], (((1,), (1,)), ((), ())), preferred_element_type=F32
            )
            total = term if total is None else total + term
        for n in range(outs):
            out_ref[t * outs + n] = total[n * lanes : (n + 1) * lanes].T
        return carry

    lax.fori_loop(0, count // outs, step, 0)


def project(occ, part, basis, pot, group):
    _, slots, _ = occ.shape
    rows, points = basis.shape
    nv = pot.shape[0]
    half = slots // 2
    return pl.pallas_call(
        functools.partial(project_kernel, start=part * half, group=group),
        in_specs=[WHOLE] * 3,
        out_specs=WHOLE,
        out_shape=jax.ShapeDtypeStruct((half // group, nv, group * rows), F32),
        cost_estimate=pl.CostEstimate(
            flops=2 * half * rows * points * nv, bytes_accessed=4_000_000, transcendentals=0
        ),
        compiler_params=ROOM,
        name="project",
    )(occ, basis, pot)


def respond_kernel(*refs, group):
    *occ_refs, basis_ref, far_ref, near_ref, out_ref = refs
    blocks, _, nv, _ = far_ref.shape
    owners, size, side = out_ref.shape
    per_owner = nv // owners
    per_step = 8

    def step(t, carry):
        lines = []
        for r in range(per_step):
            k = t * per_step + r
            cut = pl.ds(pl.multiple_of(k * side, side), side)
            parts = halves(basis_ref, cut)
            total = None
            for p, occ_ref in enumerate(occ_refs):
                occ = occ_ref[k]
                for h, ref in enumerate((far_ref, near_ref)):
                    for b in range(blocks):
                        base = (h * blocks + b) * group
                        places = range(base, base + group)
                        pairs = products(occ, places, parts[:: 1 - 2 * p])
                        term = jnp.dot(ref[b, p], pairs, preferred_element_type=F32)
                        total = term if total is None else total + term
            lines.append(total)
        rows = per_step * per_owner
        for n in range(owners):
            piece = [line[n * per_owner : (n + 1) * per_owner] for line in lines]
            piece = jnp.concatenate(piece, axis=0).astype(out_ref.dtype)
            out_ref[n, pl.ds(pl.multiple_of(t * rows, rows), rows), :] = piece
        return carry

    lax.fori_loop(0, size // per_owner // per_step, step, 0)


def respond(occs, basis, far, near, group, owners):
    lines, slots, _ = occs[0].shape
    rows, points = basis.shape
    nv = far.shape[2]
    return pl.pallas_call(
        functools.partial(respond_kernel, group=group),
        in_specs=[WHOLE] * (len(occs) + 3),
        out_specs=WHOLE,
        out_shape=jax.ShapeDtypeStruct((owners, lines * nv // owners, SIDE), BF16),
        cost_estimate=pl.CostEstimate(
            flops=2 * len(occs) * slots * rows * points * nv,
            bytes_accessed=6_000_000,
            transcendentals=0,
        ),
        compiler_params=ROOM,
        name="respond",
    )(*occs, basis, far, near)


def columns_kernel(parts_ref, cols_ref, out_ref):
    copies, count, lines, side = out_ref.shape
    size = count * lines
    plane = parts_ref[0].astype(F32)
    for s in range(1, parts_ref.shape[0]):
        plane = plane + parts_ref[s].astype(F32)
    mixed = lax.dot_general(
        plane, cols_ref[...], (((1,), (1,)), ((), ())), precision=HIGH, preferred_element_type=F32
    ).astype(BF16)
    row = lax.broadcasted_iota(jnp.int32, (size, size), 0)
    column = lax.broadcasted_iota(jnp.int32, (size, size), 1)
    source = row % lines * count + row // lines
    swap = jnp.where(source == column, 1.0, 0.0).astype(BF16)
    block = jnp.dot(swap, mixed, preferred_element_type=F32).astype(BF16)
    block = block.reshape(count, lines, side)
    for n in range(copies):
        out_ref[n] = block


def in_three(block):
    high = block.astype(BF16)
    rest = block - high.astype(F32)
    mid = rest.astype(BF16)
    low = (rest - mid.astype(F32)).astype(BF16)
    return high, mid, low


def rows_kernel(near_ref, far_ref, mix_near_ref, mix_far_ref, out_ref):
    chips, count, lines, _ = near_ref.shape
    mixes = [jnp.concatenate(in_three(m[...]), axis=0) for m in (mix_near_ref, mix_far_ref)]
    for n in range(count):
        total = None
        for ref, mix in zip((near_ref, far_ref), mixes):
            block = jnp.concatenate([ref[k, n] for k in range(chips)], axis=0)
            term = jnp.dot(mix, block, preferred_element_type=F32)
            total = term if total is None else total + term
        out_ref[n] = total[:lines] + (total[lines : 2 * lines] + total[2 * lines :])


def small_call(kernel, out, *args):
    return pl.pallas_call(kernel, out_shape=out, compiler_params=ROOM)(*args)


def body(potentials, orbitals, levels, occ_index, coul_rows, coul_cols):
    nv, points = potentials.shape
    mine = orbitals.shape[0]
    norb, nocc = levels.shape[0], occ_index.shape[0]
    nz, nx, ny, nl, nc = (lax.axis_size(a) for a in (Z, XH, Y, XL, CORE))
    z, xh, y, xl, core = (lax.axis_index(a) for a in (Z, XH, Y, XL, CORE))
    chips = ny * nl
    chip = y * nl + xl
    width = points // (nz * nx)
    slots = nocc // nx
    half = slots // nc
    group = half // chips
    lines = points // SIDE
    volume = points * chips * nc
    per_owner = nv // (nz * nx)

    blocks = jax.ShapeDtypeStruct((nz * nx, mine, width), BF16)
    partner = swapped(orbitals, XH)
    by_points = exchanged(small_call(split_kernel, blocks, orbitals), ORB)

    def part_of(values, start, count):
        return lax.dynamic_slice_in_dim(values, start, count)

    starts = [s * slots + c * half for s in range(nx) for c in (1 - core, core)]
    wanted = jnp.concatenate([part_of(occ_index, s, half) for s in starts])[:, None]
    copies = jax.ShapeDtypeStruct((nz * nx, slots, width), BF16)
    spread = small_call(pick_kernel, copies, wanted, by_points.reshape(norb, width))
    occ = exchanged(spread, ORB)

    place = jnp.arange(nv, dtype=jnp.int32)
    side = (xh + 1 + place // (nz * per_owner)) % nx
    source = (place // per_owner % nz * nx + side) * per_owner + place % per_owner
    out = jax.ShapeDtypeStruct(potentials.shape, BF16)
    pot = small_call(order_kernel, out, source[:, None], potentials)

    labels = jnp.arange(norb, dtype=jnp.int32)
    empty = 1.0 - jnp.any(occ_index[:, None] == labels[None, :], axis=0).astype(F32)
    own_slots = part_of(occ_index, xh * slots + core * half + chip * group, group)
    own_levels = jnp.sum(
        jnp.where(own_slots[:, None] == labels[None, :], levels[None, :], 0.0), axis=1
    )
    stored = [(z * nx + n) * mine for n in (xh, 1 - xh)]
    basis_empty = jnp.concatenate([part_of(empty, n, mine) for n in stored])
    basis_levels = jnp.concatenate([part_of(levels, n, mine) for n in stored])
    weight = -2.0 * basis_empty[None, :] / (own_levels[:, None] + basis_levels[None, :])
    weight = (weight / volume).reshape(1, group * nx * mine)

    my_rows = part_of(coul_rows, (chip * nc + core) * lines, lines)
    my_rows = my_rows.reshape(lines, chips, nc, lines)
    mixes = [
        lax.dynamic_index_in_dim(my_rows, c, 2, keepdims=False).reshape(lines, chips * lines)
        for c in (core, 1 - core)
    ]
    out = jax.ShapeDtypeStruct((nx * mine, points), BF16)
    bases = small_call(stack_kernel, [out] * 3, orbitals, partner)
    early = (occ, bases, pot, weight, mixes)
    occ, bases, pot, weight, mixes = lax.optimization_barrier(early)

    other_occ = swapped(occ, XH)
    far = project(occ, 0, bases[0], pot, group)
    far = swapped(far, CORE)
    near = project(occ, 1, bases[1], pot, group)
    near, other_occ = lax.optimization_barrier((near, other_occ))
    summed = small_call(join_kernel, jax.ShapeDtypeStruct(near.shape, BF16), near, far)
    intersection = jnp.sum(exchanged(summed, CHIP).astype(F32), axis=0)
    guess = (intersection * weight).astype(BF16)

    given, kept = guess[: nv // nx], guess[nv // nx :]
    guesses = jnp.stack([kept, swapped(given, XH)])
    near_guess = exchanged(jnp.broadcast_to(guesses, (chips, *guesses.shape)), CHIP)
    far_guess = swapped(near_guess, CORE)
    response = respond((occ, other_occ), bases[2], far_guess, near_guess, group, nz)

    out = jax.ShapeDtypeStruct((chips, per_owner, lines, SIDE), BF16)
    columns = small_call(columns_kernel, out, exchanged(response, Z), coul_cols)
    near_cols = exchanged(columns, CHIP)
    far_cols = swapped(near_cols, CORE)
    out = jax.ShapeDtypeStruct((per_owner, lines, SIDE), F32)
    return small_call(rows_kernel, out, near_cols, far_cols, *mixes)


def solution(mesh):
    torus = Mesh(mesh.devices.reshape(8, 2, 4, 2, 2), (Z, XH, Y, XL, CORE))
    return jax.shard_map(
        body,
        mesh=torus,
        in_specs=(P(None, CELL), P(ORB, CELL), P(), P(), P(), P()),
        out_specs=P(ORB, CELL, None),
        check_vma=False,
    )
```

profile of v0, /device:TPU:1, one launch (start us, length us, event | category | flops | bytes accessed | tf_op | source)
XLA Modules:
  0.0 169.6 jit_solution(8373849773948303896)
XLA Ops:
  0.0 1.0 copy-done.2
  1.0 0.7 shard_map.64
  1.7 11.7 %all-to-all-start = ((bf16[16,32,256]{2,1,0:T(8,128)(2,1)}), bf16[16,32,256]{2,1,0:T(8,128)(2,1)S(1)}, u32[]{:S(2)}, u32[]{:S(2)}) async-start(bf16[16,32,256]{2,1,0:T(8,128)(2,1)} %shard_map.64), calls=%async_computation | async-start | bytes 524288 | tf_op jit(solution)/shard_map/all_to_all | solution.py:28
  13.4 2.9 %collective-permute-start = (bf16[32,4096]{1,0:T(8,128)(2,1)}, bf16[32,4096]{1,0:T(8,128)(2,1)}, u32[]{:S(2)}, u32[]{:S(2)}) collective-permute-start(bf16[32,4096]{1,0:T(8,128)(2,1)} %first_ref.1), channel_id=1, source_target_pairs={{0,16},{16,0},{1,17},{17,1},{2,18},{18,2},{3,19},{19,3},{4,20},{20... | collective-permute-start | bytes 786440 | tf_op jit(solution)/shard_map/ppermute | solution.py:24
  16.3 0.9 fusion.19
  17.4 0.8 fusion
  18.2 7.4 %all-to-all-done = bf16[16,32,256]{2,1,0:T(8,128)(2,1)S(1)} async-done(((bf16[16,32,256]{2,1,0:T(8,128)(2,1)}), bf16[16,32,256]{2,1,0:T(8,128)(2,1)S(1)}, u32[]{:S(2)}, u32[]{:S(2)}) %all-to-all-start) | async-done | bytes 262176 | tf_op jit(solution)/shard_map/all_to_all | solution.py:28
  25.5 1.0 shard_map.65
  26.5 4.2 %all-to-all-start.1 = ((bf16[16,64,256]{2,1,0:T(8,128)(2,1)}), bf16[16,64,256]{2,1,0:T(8,128)(2,1)}, u32[]{:S(2)}, u32[]{:S(2)}) async-start(bf16[16,64,256]{2,1,0:T(8,128)(2,1)} %shard_map.65), calls=%async_computation.1 | async-start | bytes 1048576 | tf_op jit(solution)/shard_map/all_to_all | solution.py:28
  31.7 0.4 dynamic-slice_reduce_fusion
  32.4 0.6 shard_map.67.pot_ref
  33.4 1.1 shard_map.66
  34.5 0.8 copy-done.5
  35.3 0.8 copy-done.7
  36.1 10.4 %all-to-all-done.1.occ_ref.refs_0_ = bf16[16,64,256]{2,1,0:T(8,128)(2,1)} async-done(((bf16[16,64,256]{2,1,0:T(8,128)(2,1)}), bf16[16,64,256]{2,1,0:T(8,128)(2,1)}, u32[]{:S(2)}, u32[]{:S(2)}) %all-to-all-start.1) | async-done | bytes 524320 | tf_op jit(solution)/shard_map/all_to_all | solution.py:28
  46.5 5.9 %project.3 = f32[8,192,256]{2,1,0:T(8,128)S(1)} custom-call(bf16[16,64,256]{2,1,0:T(8,128)(2,1)} %all-to-all-done.1.occ_ref.refs_0_, bf16[64,4096]{1,0:T(8,128)(2,1)S(1)} %get-tuple-element.27.basis_ref, bf16[192,4096]{1,0:T(8,128)(2,1)S(1)} %shard_map.67.pot_ref), custom_call_target="tpu_custom_call" | custom-call | flops 3221225472 | bytes 4000000 | tf_op jit(solution)/shard_map/project/pallas_call | solution.py:104
  52.4 4.7 %collective-permute-start.2 = (f32[8,192,256]{2,1,0:T(8,128)S(1)}, f32[8,192,256]{2,1,0:T(8,128)S(1)}, u32[]{:S(2)}, u32[]{:S(2)}) collective-permute-start(f32[8,192,256]{2,1,0:T(8,128)S(1)} %project.3), channel_id=1, source_target_pairs={{0,1},{1,0},{2,3},{3,2},{4,5},{5,4},{6,7},{7,6},{8,9},{9,8},{10,11... | collective-permute-start | bytes 4718600 | tf_op jit(solution)/shard_map/ppermute | solution.py:24
  57.4 5.9 %project.2.near_ref = f32[8,192,256]{2,1,0:T(8,128)S(1)} custom-call(bf16[16,64,256]{2,1,0:T(8,128)(2,1)} %all-to-all-done.1.occ_ref.refs_0_, bf16[64,4096]{1,0:T(8,128)(2,1)S(1)} %copy-done.8, bf16[192,4096]{1,0:T(8,128)(2,1)S(1)} %shard_map.67.pot_ref), custom_call_target="tpu_custom_call" | custom-call | flops 3221225472 | bytes 4000000 | tf_op jit(solution)/shard_map/project/pallas_call | solution.py:104
  63.3 8.9 %collective-permute-done.1.refs_1_ = bf16[16,64,256]{2,1,0:T(8,128)(2,1)S(1)} collective-permute-done((bf16[16,64,256]{2,1,0:T(8,128)(2,1)}, bf16[16,64,256]{2,1,0:T(8,128)(2,1)S(1)}, u32[]{:S(2)}, u32[]{:S(2)}) %collective-permute-start.1) | collective-permute-done | bytes 524320 | tf_op jit(solution)/shard_map/ppermute | solution.py:24
  72.4 15.8 %all_to_all.30 = bf16[8,192,256]{2,1,0:T(8,128)(2,1)S(1)} all-to-all(bf16[8,192,256]{2,1,0:T(8,128)(2,1)S(1)} %shard_map.68), channel_id=1, replica_groups=mesh['z'=8,'x_hi'=2,'y'=4,'x_lo'=2,'core'=2] {'y','x_lo'}, dimensions={0} | all-to-all | bytes 1572864 | tf_op jit(solution)/shard_map/all_to_all | solution.py:28
  88.3 1.0 collective-permute-start.3
  89.3 3.6 %collective-permute-done.3 = bf16[96,256]{1,0:T(8,128)(2,1)S(1)} collective-permute-done((bf16[96,256]{1,0:T(8,128)(2,1)S(1)}, bf16[96,256]{1,0:T(8,128)(2,1)S(1)}, u32[]{:S(2)}, u32[]{:S(2)}) %collective-permute-start.3) | collective-permute-done | bytes 49184 | tf_op jit(solution)/shard_map/ppermute | solution.py:24
  92.9 13.0 %all_to_all.31.refs_4_ = bf16[8,2,96,256]{3,2,1,0:T(8,128)(2,1)S(1)} all-to-all(bf16[8,2,96,256]{3,2,1,0:T(8,128)(2,1)S(1)} %broadcast_in_dim.30), channel_id=1, replica_groups=mesh['z'=8,'x_hi'=2,'y'=4,'x_lo'=2,'core'=2] {'y','x_lo'}, dimensions={0} | all-to-all | bytes 1572864 | tf_op jit(solution)/shard_map/all_to_all | solution.py:28
  106.0 3.7 %collective-permute-start.4 = (bf16[8,2,96,256]{3,2,1,0:T(8,128)(2,1)S(1)}, bf16[8,2,96,256]{3,2,1,0:T(8,128)(2,1)S(1)}, u32[]{:S(2)}, u32[]{:S(2)}) collective-permute-start(bf16[8,2,96,256]{3,2,1,0:T(8,128)(2,1)S(1)} %all_to_all.31.refs_4_), channel_id=1, source_target_pairs={{0,1},{1,0},{2,3},{3,2},{4,5},{5,4},{6,7},{7,6},{8,9},{9,8},{10,11... | collective-permute-start | bytes 2359304 | tf_op jit(solution)/shard_map/ppermute | solution.py:24
  109.7 1.9 %collective-permute-done.4.refs_3_ = bf16[8,2,96,256]{3,2,1,0:T(8,128)(2,1)S(1)} collective-permute-done((bf16[8,2,96,256]{3,2,1,0:T(8,128)(2,1)S(1)}, bf16[8,2,96,256]{3,2,1,0:T(8,128)(2,1)S(1)}, u32[]{:S(2)}, u32[]{:S(2)}) %collective-permute-start.4) | collective-permute-done | bytes 786464 | tf_op jit(solution)/shard_map/ppermute | solution.py:24
  111.6 11.9 %respond.1 = bf16[8,192,256]{2,1,0:T(8,128)(2,1)S(1)} custom-call(bf16[16,64,256]{2,1,0:T(8,128)(2,1)} %all-to-all-done.1.occ_ref.refs_0_, bf16[16,64,256]{2,1,0:T(8,128)(2,1)S(1)} %collective-permute-done.1.refs_1_, bf16[64,4096]{1,0:T(8,128)(2,1)S(1)} %copy-done.6, bf16[8,2,96,256]{3,2,1,0:T(8,128)(2,1)S(1)} %collective-permute-done.4.refs_3_, ...), custom_call_target="tpu_custom_call" | custom-call | flops 6442450944 | bytes 6000000 | tf_op jit(solution)/shard_map/respond/pallas_call | solution.py:155
  123.5 26.1 %all_to_all.32.parts_ref = bf16[8,192,256]{2,1,0:T(8,128)(2,1)S(1)} all-to-all(bf16[8,192,256]{2,1,0:T(8,128)(2,1)S(1)} %respond.1), channel_id=1, replica_groups=mesh['z'=8,'x_hi'=2,'y'=4,'x_lo'=2,'core'=2] {'z'}, dimensions={0} | all-to-all | bytes 1572864 | tf_op jit(solution)/shard_map/all_to_all | solution.py:28
  149.7 0.7 shard_map.69
  150.4 14.6 %all_to_all.33.near_ref = bf16[8,12,16,256]{3,2,1,0:T(8,128)(2,1)S(1)} all-to-all(bf16[8,12,16,256]{3,2,1,0:T(8,128)(2,1)S(1)} %shard_map.69), channel_id=1, replica_groups=mesh['z'=8,'x_hi'=2,'y'=4,'x_lo'=2,'core'=2] {'y','x_lo'}, dimensions={0} | all-to-all | bytes 1572864 | tf_op jit(solution)/shard_map/all_to_all | solution.py:28
  164.9 1.7 %collective-permute-start.5 = (bf16[8,12,16,256]{3,2,1,0:T(8,128)(2,1)S(1)}, bf16[8,12,16,256]{3,2,1,0:T(8,128)(2,1)S(1)}, u32[]{:S(2)}, u32[]{:S(2)}) collective-permute-start(bf16[8,12,16,256]{3,2,1,0:T(8,128)(2,1)S(1)} %all_to_all.33.near_ref), channel_id=1, source_target_pairs={{0,1},{1,0},{2,3},{3,2},{4,5},{5,4},{6,7},{7,6},{8,9},{9,8},{10,11... | collective-permute-start | bytes 2359304 | tf_op jit(solution)/shard_map/ppermute | solution.py:24
  166.6 1.9 %collective-permute-done.5.far_ref = bf16[8,12,16,256]{3,2,1,0:T(8,128)(2,1)S(1)} collective-permute-done((bf16[8,12,16,256]{3,2,1,0:T(8,128)(2,1)S(1)}, bf16[8,12,16,256]{3,2,1,0:T(8,128)(2,1)S(1)}, u32[]{:S(2)}, u32[]{:S(2)}) %collective-permute-start.5) | collective-permute-done | bytes 786464 | tf_op jit(solution)/shard_map/ppermute | solution.py:24
  168.5 1.0 shard_map.70
  (43 shorter events, 2.4 us)
Async XLA Ops:
  0.0 31.5 %copy-start = (f32[256,256]{1,0:T(8,128)S(1)}, f32[256,256]{1,0:T(8,128)}, u32[]{:S(2)}) copy-start(f32[256,256]{1,0:T(8,128)} %param.10) | copy-start | bytes 786436
  0.0 1.0 copy-start.2
  1.0 29.8 %copy-start.9 = (s32[128]{0:T(128)S(1)}, s32[128]{0:T(128)}, u32[]{:S(2)}) copy-start(s32[128]{0:T(128)} %param.9) | copy-start | bytes 1540
  1.0 29.9 %copy-start.10 = (f32[512]{0:T(512)S(1)}, f32[512]{0:T(512)}, u32[]{:S(2)}) copy-start(f32[512]{0:T(512)} %param.8) | copy-start | bytes 6148
  1.7 30.7 %copy-start.1 = (bf16[192,4096]{1,0:T(8,128)(2,1)S(1)}, bf16[192,4096]{1,0:T(8,128)(2,1)}, u32[]{:S(2)}) copy-start(bf16[192,4096]{1,0:T(8,128)(2,1)} %rows_ref.3) | copy-start | bytes 4718596
  1.7 23.8 %all-to-all-start = ((bf16[16,32,256]{2,1,0:T(8,128)(2,1)}), bf16[16,32,256]{2,1,0:T(8,128)(2,1)S(1)}, u32[]{:S(2)}, u32[]{:S(2)}) async-start(bf16[16,32,256]{2,1,0:T(8,128)(2,1)} %shard_map.64), calls=%async_computation | async-start | bytes 524288 | tf_op jit(solution)/shard_map/all_to_all | solution.py:28
  13.4 19.6 %collective-permute-start = (bf16[32,4096]{1,0:T(8,128)(2,1)}, bf16[32,4096]{1,0:T(8,128)(2,1)}, u32[]{:S(2)}, u32[]{:S(2)}) collective-permute-start(bf16[32,4096]{1,0:T(8,128)(2,1)} %first_ref.1), channel_id=1, source_target_pairs={{0,16},{16,0},{1,17},{17,1},{2,18},{18,2},{3,19},{19,3},{4,20},{20... | collective-permute-start | bytes 786440 | tf_op jit(solution)/shard_map/ppermute | solution.py:24
  26.5 20.0 %all-to-all-start.1 = ((bf16[16,64,256]{2,1,0:T(8,128)(2,1)}), bf16[16,64,256]{2,1,0:T(8,128)(2,1)}, u32[]{:S(2)}, u32[]{:S(2)}) async-start(bf16[16,64,256]{2,1,0:T(8,128)(2,1)} %shard_map.65), calls=%async_computation.1 | async-start | bytes 1048576 | tf_op jit(solution)/shard_map/all_to_all | solution.py:28
  32.4 1.0 copy-start.3
  34.4 0.8 copy-start.5
  35.3 0.8 copy-start.7
  46.5 10.9 %copy-start.8 = (bf16[64,4096]{1,0:T(8,128)(2,1)S(1)}, bf16[64,4096]{1,0:T(8,128)(2,1)}, u32[]{:S(2)}) copy-start(bf16[64,4096]{1,0:T(8,128)(2,1)} %copy-done.7) | copy-start | bytes 1572868
  52.4 19.8 %collective-permute-start.2 = (f32[8,192,256]{2,1,0:T(8,128)S(1)}, f32[8,192,256]{2,1,0:T(8,128)S(1)}, u32[]{:S(2)}, u32[]{:S(2)}) collective-permute-start(f32[8,192,256]{2,1,0:T(8,128)S(1)} %project.3), channel_id=1, source_target_pairs={{0,1},{1,0},{2,3},{3,2},{4,5},{5,4},{6,7},{7,6},{8,9},{9,8},{10,11... | collective-permute-start | bytes 4718600 | tf_op jit(solution)/shard_map/ppermute | solution.py:24
  57.2 15.1 %collective-permute-start.1 = (bf16[16,64,256]{2,1,0:T(8,128)(2,1)}, bf16[16,64,256]{2,1,0:T(8,128)(2,1)S(1)}, u32[]{:S(2)}, u32[]{:S(2)}) collective-permute-start(bf16[16,64,256]{2,1,0:T(8,128)(2,1)} %all-to-all-done.1.occ_ref.refs_0_), channel_id=1, source_target_pairs={{0,16},{16,0},{1,17},{17,1},{2,18},{18,2},{3,19},{19,3},{4,20},{20... | collective-permute-start | bytes 1572872 | tf_op jit(solution)/shard_map/ppermute | solution.py:24
  88.3 23.4 %copy-start.6 = (bf16[64,4096]{1,0:T(8,128)(2,1)S(1)}, bf16[64,4096]{1,0:T(8,128)(2,1)}, u32[]{:S(2)}) copy-start(bf16[64,4096]{1,0:T(8,128)(2,1)} %copy-done.5) | copy-start | bytes 1572868
  88.3 4.5 %collective-permute-start.3 = (bf16[96,256]{1,0:T(8,128)(2,1)S(1)}, bf16[96,256]{1,0:T(8,128)(2,1)S(1)}, u32[]{:S(2)}, u32[]{:S(2)}) collective-permute-start(bf16[96,256]{1,0:T(8,128)(2,1)S(1)} %get-tuple-element.34), channel_id=1, source_target_pairs={{0,16},{16,0},{1,17},{17,1},{2,18},{18,2},{3,19},{19,3},{4,20},{20... | collective-permute-start | bytes 147464 | tf_op jit(solution)/shard_map/ppermute | solution.py:24
  106.0 5.7 %collective-permute-start.4 = (bf16[8,2,96,256]{3,2,1,0:T(8,128)(2,1)S(1)}, bf16[8,2,96,256]{3,2,1,0:T(8,128)(2,1)S(1)}, u32[]{:S(2)}, u32[]{:S(2)}) collective-permute-start(bf16[8,2,96,256]{3,2,1,0:T(8,128)(2,1)S(1)} %all_to_all.31.refs_4_), channel_id=1, source_target_pairs={{0,1},{1,0},{2,3},{3,2},{4,5},{5,4},{6,7},{7,6},{8,9},{9,8},{10,11... | collective-permute-start | bytes 2359304 | tf_op jit(solution)/shard_map/ppermute | solution.py:24
  123.5 26.2 %copy-start.4 = (f32[256,256]{1,0:T(8,128)S(1)}, f32[256,256]{1,0:T(8,128)}, u32[]{:S(2)}) copy-start(f32[256,256]{1,0:T(8,128)} %cols_ref.1) | copy-start | bytes 786436
  164.9 3.6 %collective-permute-start.5 = (bf16[8,12,16,256]{3,2,1,0:T(8,128)(2,1)S(1)}, bf16[8,12,16,256]{3,2,1,0:T(8,128)(2,1)S(1)}, u32[]{:S(2)}, u32[]{:S(2)}) collective-permute-start(bf16[8,12,16,256]{3,2,1,0:T(8,128)(2,1)S(1)} %all_to_all.33.near_ref), channel_id=1, source_target_pairs={{0,1},{1,0},{2,3},{3,2},{4,5},{5,4},{6,7},{7,6},{8,9},{9,8},{10,11... | collective-permute-start | bytes 2359304 | tf_op jit(solution)/shard_map/ppermute | solution.py:24
where the time goes:
time: 170 us
  blocking collectives  69.5 us (41%)
  waiting for transfers between devices  34.1 us (20%)
  starting transfers between devices  30.2 us (18%)
  Pallas kernels  28.9 us (17%)
  local copies, waits for them, and re-layouts  5.05 us (3%)
    all_to_all x4, blocking collectives, exchanged(): return lax.all_to_all(parts, axes, split_axis=0, concat_axis=0, tiled=True)  69.5 us
    all_to_all x2, waiting for transfers between devices, exchanged(): return lax.all_to_all(parts, axes, split_axis=0, concat_axis=0, tiled=True)  17.8 us
    ppermute x6, waiting for transfers between devices, swapped(): return lax.ppermute(shard, axis, SWAP)  16.3 us
    all_to_all x2, starting transfers between devices, exchanged(): return lax.all_to_all(parts, axes, split_axis=0, concat_axis=0, tiled=True)  15.9 us
    ppermute x6, starting transfers between devices, swapped(): return lax.ppermute(shard, axis, SWAP)  14.3 us
    pallas_call x1, Pallas kernels, respond(): pl.pallas_call(functools.partial(respond_kernel, group=group), in_specs=[...  11.9 us
    pallas_call x2, Pallas kernels, project(): pl.pallas_call(functools.partial(project_kernel, start=part * half, group...  11.8 us
    pallas_call x7, Pallas kernels, small_call(): return pl.pallas_call(kernel, out_shape=out, compiler_params=ROOM)(*args)  5.25 us
  transfers between devices with their start and end apart: 8, of which 6 were waited for; matrix products, arithmetic and copies ran while one was open for 2% of the time, Pallas kernels for 5%

commit v1 on v0

--- a/solution.py
+++ b/solution.py
@@ -28,10 +28,29 @@
     return lax.all_to_all(parts, axes, split_axis=0, concat_axis=0, tiled=True)
 
 
-def split_kernel(rows_ref, out_ref):
+def split_kernel(rows_ref, out_ref, sems):
     width = out_ref.shape[2]
-    for k in range(out_ref.shape[0]):
-        out_ref[k] = rows_ref[:, k * width : (k + 1) * width]
+    copies = [
+        pltpu.make_async_copy(rows_ref.at[:, pl.ds(k * width, width)], out_ref.at[k], sems.at[k])
+        for k in range(out_ref.shape[0])
+    ]
+    for copy in copies:
+        copy.start()
+    for copy in copies:
+        copy.wait()
+
+
+def split(rows, count):
+    dims = (count, rows.shape[0], rows.shape[1] // count)
+    return pl.pallas_call(
+        split_kernel,
+        in_specs=[pl.BlockSpec(memory_space=pl.ANY)],
+        out_specs=WHOLE,
+        out_shape=jax.ShapeDtypeStruct(dims, rows.dtype),
+        scratch_shapes=[pltpu.SemaphoreType.DMA((count,))],
+        compiler_params=pltpu.CompilerParams(vmem_limit_bytes=60 * 2**20),
+        name="split",
+    )(rows)
 
 
 def pick_kernel(wanted_ref, rows_ref, out_ref):
@@ -72,7 +91,9 @@
     return basis_ref[:rows, cut], basis_ref[rows:, cut]
 
 
-def project_kernel(occ_ref, basis_ref, pot_ref, out_ref, *, start, group):
+def project_kernel(occ_ref, basis_ref, pot_ref, out_ref, *occ_copies, start, group):
+    for ref in occ_copies:
+        ref[...] = occ_ref[...]
     blocks, _, width = occ_ref.shape
     count, _, lanes = out_ref.shape
     per_step = 16
@@ -101,11 +122,13 @@
     rows, points = basis.shape
     nv = pot.shape[0]
     half = slots // 2
+    outs = [jax.ShapeDtypeStruct((half // group, nv, group * rows), F32)]
+    outs += [jax.ShapeDtypeStruct(occ.shape, occ.dtype)] * (2 * (1 - part))
     return pl.pallas_call(
         functools.partial(project_kernel, start=part * half, group=group),
         in_specs=[WHOLE] * 3,
-        out_specs=WHOLE,
-        out_shape=jax.ShapeDtypeStruct((half // group, nv, group * rows), F32),
+        out_specs=[WHOLE] * len(outs),
+        out_shape=outs,
         cost_estimate=pl.CostEstimate(
             flops=2 * half * rows * points * nv, bytes_accessed=4_000_000, transcendentals=0
         ),
@@ -226,9 +249,8 @@
     volume = points * chips * nc
     per_owner = nv // (nz * nx)
 
-    blocks = jax.ShapeDtypeStruct((nz * nx, mine, width), BF16)
     partner = swapped(orbitals, XH)
-    by_points = exchanged(small_call(split_kernel, blocks, orbitals), ORB)
+    by_points = exchanged(split(orbitals, nz * nx), ORB)
 
     def part_of(values, start, count):
         return lax.dynamic_slice_in_dim(values, start, count)
@@ -269,9 +291,9 @@
     occ, bases, pot, weight, mixes = lax.optimization_barrier(early)
 
     other_occ = swapped(occ, XH)
-    far = project(occ, 0, bases[0], pot, group)
+    far, *occs = project(occ, 0, bases[0], pot, group)
     far = swapped(far, CORE)
-    near = project(occ, 1, bases[1], pot, group)
+    (near,) = project(occs[0], 1, bases[1], pot, group)
     near, other_occ = lax.optimization_barrier((near, other_occ))
     summed = small_call(join_kernel, jax.ShapeDtypeStruct(near.shape, BF16), near, far)
     intersection = jnp.sum(exchanged(summed, CHIP).astype(F32), axis=0)
@@ -281,7 +303,7 @@
     guesses = jnp.stack([kept, swapped(given, XH)])
     near_guess = exchanged(jnp.broadcast_to(guesses, (chips, *guesses.shape)), CHIP)
     far_guess = swapped(near_guess, CORE)
-    response = respond((occ, other_occ), bases[2], far_guess, near_guess, group, nz)
+    response = respond((occs[1], other_occ), bases[2], far_guess, near_guess, group, nz)
 
     out = jax.ShapeDtypeStruct((chips, per_owner, lines, SIDE), BF16)
     columns = small_call(columns_kernel, out, exchanged(response, Z), coul_cols)

time: 170 us -> 169 us (level)
    pallas_call x0 -> x1, Pallas kernels: none -> 1.75 us  [split(): pl.pallas_call(split_kernel, in_specs=[pl.BlockSpec(memory_space=pl.ANY)]...]
    pallas_call x7 -> x6, Pallas kernels: 5.25 us -> 4.53 us  [small_call(): return pl.pallas_call(kernel, out_shape=out, compiler_params=ROOM)(*args)]
  transfers between devices with their start and end apart: 8 -> 8, of which waited for: 6 -> 6; matrix products, arithmetic and copies ran while one was open for 2% -> 2% of each run, Pallas kernels for 5% -> 4%
where the time goes in v1:
time: 169 us
  blocking collectives  69.3 us (41%)
  waiting for transfers between devices  35.2 us (21%)
  starting transfers between devices  30.4 us (18%)
  Pallas kernels  27.9 us (17%)
  local copies, waits for them, and re-layouts  4.06 us (2%)
    all_to_all x4, blocking collectives, exchanged(): return lax.all_to_all(parts, axes, split_axis=0, concat_axis=0, tiled=True)  69.3 us
    all_to_all x2, waiting for transfers between devices, exchanged(): return lax.all_to_all(parts, axes, split_axis=0, concat_axis=0, tiled=True)  17.8 us
    ppermute x6, waiting for transfers between devices, swapped(): return lax.ppermute(shard, axis, SWAP)  17.4 us
    all_to_all x2, starting transfers between devices, exchanged(): return lax.all_to_all(parts, axes, split_axis=0, concat_axis=0, tiled=True)  15.9 us
    ppermute x6, starting transfers between devices, swapped(): return lax.ppermute(shard, axis, SWAP)  14.5 us
    pallas_call x1, Pallas kernels, respond(): pl.pallas_call(functools.partial(respond_kernel, group=group), in_specs=[...  10.8 us
    pallas_call x2, Pallas kernels, project(): pl.pallas_call(functools.partial(project_kernel, start=part * half, group...  10.8 us
    pallas_call x6, Pallas kernels, small_call(): return pl.pallas_call(kernel, out_shape=out, compiler_params=ROOM)(*args)  4.53 us
  transfers between devices with their start and end apart: 8, of which 6 were waited for; matrix products, arithmetic and copies ran while one was open for 2% of the time, Pallas kernels for 4%

profile of v1, /device:TPU:1, one launch (start us, length us, event | category | flops | bytes accessed | tf_op | source)
XLA Modules:
  0.0 168.6 jit_solution(6638403534749221087)
XLA Ops:
  0.0 1.8 %split.1 = bf16[16,32,256]{2,1,0:T(8,128)(2,1)} custom-call(bf16[32,4096]{1,0:T(8,128)(2,1)} %first_ref.1), custom_call_target="tpu_custom_call" | custom-call | tf_op jit(solution)/shard_map/split/pallas_call | solution.py:45
  1.8 11.7 %all-to-all-start = ((bf16[16,32,256]{2,1,0:T(8,128)(2,1)}), bf16[16,32,256]{2,1,0:T(8,128)(2,1)S(1)}, u32[]{:S(2)}, u32[]{:S(2)}) async-start(bf16[16,32,256]{2,1,0:T(8,128)(2,1)} %split.1), calls=%async_computation | async-start | bytes 524288 | tf_op jit(solution)/shard_map/all_to_all | solution.py:28
  13.5 2.9 %collective-permute-start = (bf16[32,4096]{1,0:T(8,128)(2,1)}, bf16[32,4096]{1,0:T(8,128)(2,1)}, u32[]{:S(2)}, u32[]{:S(2)}) collective-permute-start(bf16[32,4096]{1,0:T(8,128)(2,1)} %first_ref.1), channel_id=1, source_target_pairs={{0,16},{16,0},{1,17},{17,1},{2,18},{18,2},{3,19},{19,3},{4,20},{20... | collective-permute-start | bytes 786440 | tf_op jit(solution)/shard_map/ppermute | solution.py:24
  16.4 0.9 fusion.19
  17.4 0.8 fusion
  18.2 7.4 %all-to-all-done = bf16[16,32,256]{2,1,0:T(8,128)(2,1)S(1)} async-done(((bf16[16,32,256]{2,1,0:T(8,128)(2,1)}), bf16[16,32,256]{2,1,0:T(8,128)(2,1)S(1)}, u32[]{:S(2)}, u32[]{:S(2)}) %all-to-all-start) | async-done | bytes 262176 | tf_op jit(solution)/shard_map/all_to_all | solution.py:28
  25.6 1.0 shard_map.64
  26.6 4.2 %all-to-all-start.1 = ((bf16[16,64,256]{2,1,0:T(8,128)(2,1)}), bf16[16,64,256]{2,1,0:T(8,128)(2,1)}, u32[]{:S(2)}, u32[]{:S(2)}) async-start(bf16[16,64,256]{2,1,0:T(8,128)(2,1)} %shard_map.64), calls=%async_computation.1 | async-start | bytes 1048576 | tf_op jit(solution)/shard_map/all_to_all | solution.py:28
  31.8 0.4 dynamic-slice_reduce_fusion
  32.5 0.6 shard_map.66.pot_ref
  33.1 0.3 copy-done.2
  33.5 1.1 shard_map.65
  34.5 0.8 copy-done.4
  35.3 0.8 copy-done.6
  36.1 10.4 %all-to-all-done.1.occ_ref = bf16[16,64,256]{2,1,0:T(8,128)(2,1)} async-done(((bf16[16,64,256]{2,1,0:T(8,128)(2,1)}), bf16[16,64,256]{2,1,0:T(8,128)(2,1)}, u32[]{:S(2)}, u32[]{:S(2)}) %all-to-all-start.1) | async-done | bytes 524320 | tf_op jit(solution)/shard_map/all_to_all | solution.py:28
  46.6 6.0 %project.2 = (f32[8,192,256]{2,1,0:T(8,128)S(1)}, bf16[16,64,256]{2,1,0:T(8,128)(2,1)S(1)}, bf16[16,64,256]{2,1,0:T(8,128)(2,1)S(1)}) custom-call(bf16[16,64,256]{2,1,0:T(8,128)(2,1)} %all-to-all-done.1.occ_ref, bf16[64,4096]{1,0:T(8,128)(2,1)S(1)} %get-tuple-element.25.basis_ref, bf16[192,4096]{1,0:T(8,128)(2,1)S(1)} %shard_map.66.pot_ref), custom_call_target="tpu_custom_call" | custom-call | flops 3221225472 | bytes 4000000 | tf_op jit(solution)/shard_map/project/pallas_call | solution.py:127
  52.6 4.7 %collective-permute-start.2 = (f32[8,192,256]{2,1,0:T(8,128)S(1)}, f32[8,192,256]{2,1,0:T(8,128)S(1)}, u32[]{:S(2)}, u32[]{:S(2)}) collective-permute-start(f32[8,192,256]{2,1,0:T(8,128)S(1)} %get-tuple-element.33), channel_id=1, source_target_pairs={{0,1},{1,0},{2,3},{3,2},{4,5},{5,4},{6,7},{7,6},{8,9},{9,8},{10,11... | collective-permute-start | bytes 4718600 | tf_op jit(solution)/shard_map/ppermute | solution.py:24
  57.6 4.8 %project.3.near_ref = f32[8,192,256]{2,1,0:T(8,128)S(1)} custom-call(bf16[16,64,256]{2,1,0:T(8,128)(2,1)S(1)} %get-tuple-element.28.occ_ref, bf16[64,4096]{1,0:T(8,128)(2,1)S(1)} %copy-done.7, bf16[192,4096]{1,0:T(8,128)(2,1)S(1)} %shard_map.66.pot_ref), custom_call_target="tpu_custom_call" | custom-call | flops 3221225472 | bytes 4000000 | tf_op jit(solution)/shard_map/project/pallas_call | solution.py:127
  62.4 10.0 %collective-permute-done.1.refs_1_ = bf16[16,64,256]{2,1,0:T(8,128)(2,1)S(1)} collective-permute-done((bf16[16,64,256]{2,1,0:T(8,128)(2,1)}, bf16[16,64,256]{2,1,0:T(8,128)(2,1)S(1)}, u32[]{:S(2)}, u32[]{:S(2)}) %collective-permute-start.1) | collective-permute-done | bytes 524320 | tf_op jit(solution)/shard_map/ppermute | solution.py:24
  72.5 15.8 %all_to_all.30 = bf16[8,192,256]{2,1,0:T(8,128)(2,1)S(1)} all-to-all(bf16[8,192,256]{2,1,0:T(8,128)(2,1)S(1)} %shard_map.67), channel_id=1, replica_groups=mesh['z'=8,'x_hi'=2,'y'=4,'x_lo'=2,'core'=2] {'y','x_lo'}, dimensions={0} | all-to-all | bytes 1572864 | tf_op jit(solution)/shard_map/all_to_all | solution.py:28
  88.5 1.0 collective-permute-start.3
  89.4 3.6 %collective-permute-done.3 = bf16[96,256]{1,0:T(8,128)(2,1)S(1)} collective-permute-done((bf16[96,256]{1,0:T(8,128)(2,1)S(1)}, bf16[96,256]{1,0:T(8,128)(2,1)S(1)}, u32[]{:S(2)}, u32[]{:S(2)}) %collective-permute-start.3) | collective-permute-done | bytes 49184 | tf_op jit(solution)/shard_map/ppermute | solution.py:24
  93.1 13.0 %all_to_all.31.refs_4_ = bf16[8,2,96,256]{3,2,1,0:T(8,128)(2,1)S(1)} all-to-all(bf16[8,2,96,256]{3,2,1,0:T(8,128)(2,1)S(1)} %broadcast_in_dim.30), channel_id=1, replica_groups=mesh['z'=8,'x_hi'=2,'y'=4,'x_lo'=2,'core'=2] {'y','x_lo'}, dimensions={0} | all-to-all | bytes 1572864 | tf_op jit(solution)/shard_map/all_to_all | solution.py:28
  106.1 3.7 %collective-permute-start.4 = (bf16[8,2,96,256]{3,2,1,0:T(8,128)(2,1)S(1)}, bf16[8,2,96,256]{3,2,1,0:T(8,128)(2,1)S(1)}, u32[]{:S(2)}, u32[]{:S(2)}) collective-permute-start(bf16[8,2,96,256]{3,2,1,0:T(8,128)(2,1)S(1)} %all_to_all.31.refs_4_), channel_id=1, source_target_pairs={{0,1},{1,0},{2,3},{3,2},{4,5},{5,4},{6,7},{7,6},{8,9},{9,8},{10,11... | collective-permute-start | bytes 2359304 | tf_op jit(solution)/shard_map/ppermute | solution.py:24
  109.9 1.9 %collective-permute-done.4.refs_3_ = bf16[8,2,96,256]{3,2,1,0:T(8,128)(2,1)S(1)} collective-permute-done((bf16[8,2,96,256]{3,2,1,0:T(8,128)(2,1)S(1)}, bf16[8,2,96,256]{3,2,1,0:T(8,128)(2,1)S(1)}, u32[]{:S(2)}, u32[]{:S(2)}) %collective-permute-start.4) | collective-permute-done | bytes 786464 | tf_op jit(solution)/shard_map/ppermute | solution.py:24
  111.8 10.8 %respond.1 = bf16[8,192,256]{2,1,0:T(8,128)(2,1)S(1)} custom-call(bf16[16,64,256]{2,1,0:T(8,128)(2,1)S(1)} %get-tuple-element.27.refs_0_, bf16[16,64,256]{2,1,0:T(8,128)(2,1)S(1)} %collective-permute-done.1.refs_1_, bf16[64,4096]{1,0:T(8,128)(2,1)S(1)} %copy-done.5, bf16[8,2,96,256]{3,2,1,0:T(8,128)(2,1)S(1)} %collective-permute-done.4.refs_3_, ...), custom_call_target="tpu_custom_call" | custom-call | flops 6442450944 | bytes 6000000 | tf_op jit(solution)/shard_map/respond/pallas_call | solution.py:178
  122.6 26.1 %all_to_all.32.parts_ref = bf16[8,192,256]{2,1,0:T(8,128)(2,1)S(1)} all-to-all(bf16[8,192,256]{2,1,0:T(8,128)(2,1)S(1)} %respond.1), channel_id=1, replica_groups=mesh['z'=8,'x_hi'=2,'y'=4,'x_lo'=2,'core'=2] {'z'}, dimensions={0} | all-to-all | bytes 1572864 | tf_op jit(solution)/shard_map/all_to_all | solution.py:28
  148.7 0.7 shard_map.68
  149.3 14.4 %all_to_all.33.near_ref = bf16[8,12,16,256]{3,2,1,0:T(8,128)(2,1)S(1)} all-to-all(bf16[8,12,16,256]{3,2,1,0:T(8,128)(2,1)S(1)} %shard_map.68), channel_id=1, replica_groups=mesh['z'=8,'x_hi'=2,'y'=4,'x_lo'=2,'core'=2] {'y','x_lo'}, dimensions={0} | all-to-all | bytes 1572864 | tf_op jit(solution)/shard_map/all_to_all | solution.py:28
  163.8 1.9 %collective-permute-start.5 = (bf16[8,12,16,256]{3,2,1,0:T(8,128)(2,1)S(1)}, bf16[8,12,16,256]{3,2,1,0:T(8,128)(2,1)S(1)}, u32[]{:S(2)}, u32[]{:S(2)}) collective-permute-start(bf16[8,12,16,256]{3,2,1,0:T(8,128)(2,1)S(1)} %all_to_all.33.near_ref), channel_id=1, source_target_pairs={{0,1},{1,0},{2,3},{3,2},{4,5},{5,4},{6,7},{7,6},{8,9},{9,8},{10,11... | collective-permute-start | bytes 2359304 | tf_op jit(solution)/shard_map/ppermute | solution.py:24
  165.6 1.9 %collective-permute-done.5.far_ref = bf16[8,12,16,256]{3,2,1,0:T(8,128)(2,1)S(1)} collective-permute-done((bf16[8,12,16,256]{3,2,1,0:T(8,128)(2,1)S(1)}, bf16[8,12,16,256]{3,2,1,0:T(8,128)(2,1)S(1)}, u32[]{:S(2)}, u32[]{:S(2)}) %collective-permute-start.5) | collective-permute-done | bytes 786464 | tf_op jit(solution)/shard_map/ppermute | solution.py:24
  167.5 1.0 shard_map.69
  (41 shorter events, 2.0 us)
Async XLA Ops:
  0.0 31.5 %copy-start = (f32[256,256]{1,0:T(8,128)S(1)}, f32[256,256]{1,0:T(8,128)}, u32[]{:S(2)}) copy-start(f32[256,256]{1,0:T(8,128)} %param.10) | copy-start | bytes 786436
  0.0 30.9 %copy-start.8 = (s32[128]{0:T(128)S(1)}, s32[128]{0:T(128)}, u32[]{:S(2)}) copy-start(s32[128]{0:T(128)} %param.9) | copy-start | bytes 1540
  0.0 30.9 %copy-start.9 = (f32[512]{0:T(512)S(1)}, f32[512]{0:T(512)}, u32[]{:S(2)}) copy-start(f32[512]{0:T(512)} %param.8) | copy-start | bytes 6148
  1.8 30.7 %copy-start.1 = (bf16[192,4096]{1,0:T(8,128)(2,1)S(1)}, bf16[192,4096]{1,0:T(8,128)(2,1)}, u32[]{:S(2)}) copy-start(bf16[192,4096]{1,0:T(8,128)(2,1)} %rows_ref.3) | copy-start | bytes 4718596
  1.8 23.8 %all-to-all-start = ((bf16[16,32,256]{2,1,0:T(8,128)(2,1)}), bf16[16,32,256]{2,1,0:T(8,128)(2,1)S(1)}, u32[]{:S(2)}, u32[]{:S(2)}) async-start(bf16[16,32,256]{2,1,0:T(8,128)(2,1)} %split.1), calls=%async_computation | async-start | bytes 524288 | tf_op jit(solution)/shard_map/all_to_all | solution.py:28
  13.5 19.6 %collective-permute-start = (bf16[32,4096]{1,0:T(8,128)(2,1)}, bf16[32,4096]{1,0:T(8,128)(2,1)}, u32[]{:S(2)}, u32[]{:S(2)}) collective-permute-start(bf16[32,4096]{1,0:T(8,128)(2,1)} %first_ref.1), channel_id=1, source_target_pairs={{0,16},{16,0},{1,17},{17,1},{2,18},{18,2},{3,19},{19,3},{4,20},{20... | collective-permute-start | bytes 786440 | tf_op jit(solution)/shard_map/ppermute | solution.py:24
  26.6 20.0 %all-to-all-start.1 = ((bf16[16,64,256]{2,1,0:T(8,128)(2,1)}), bf16[16,64,256]{2,1,0:T(8,128)(2,1)}, u32[]{:S(2)}, u32[]{:S(2)}) async-start(bf16[16,64,256]{2,1,0:T(8,128)(2,1)} %shard_map.64), calls=%async_computation.1 | async-start | bytes 1048576 | tf_op jit(solution)/shard_map/all_to_all | solution.py:28
  32.5 1.0 copy-start.2
  34.5 0.8 copy-start.4
  35.3 0.8 copy-start.6
  46.6 11.0 %copy-start.7 = (bf16[64,4096]{1,0:T(8,128)(2,1)S(1)}, bf16[64,4096]{1,0:T(8,128)(2,1)}, u32[]{:S(2)}) copy-start(bf16[64,4096]{1,0:T(8,128)(2,1)} %copy-done.6) | copy-start | bytes 1572868
  52.6 19.8 %collective-permute-start.2 = (f32[8,192,256]{2,1,0:T(8,128)S(1)}, f32[8,192,256]{2,1,0:T(8,128)S(1)}, u32[]{:S(2)}, u32[]{:S(2)}) collective-permute-start(f32[8,192,256]{2,1,0:T(8,128)S(1)} %get-tuple-element.33), channel_id=1, source_target_pairs={{0,1},{1,0},{2,3},{3,2},{4,5},{5,4},{6,7},{7,6},{8,9},{9,8},{10,11... | collective-permute-start | bytes 4718600 | tf_op jit(solution)/shard_map/ppermute | solution.py:24
  57.3 15.1 %collective-permute-start.1 = (bf16[16,64,256]{2,1,0:T(8,128)(2,1)}, bf16[16,64,256]{2,1,0:T(8,128)(2,1)S(1)}, u32[]{:S(2)}, u32[]{:S(2)}) collective-permute-start(bf16[16,64,256]{2,1,0:T(8,128)(2,1)} %all-to-all-done.1.occ_ref), channel_id=1, source_target_pairs={{0,16},{16,0},{1,17},{17,1},{2,18},{18,2},{3,19},{19,3},{4,20},{20... | collective-permute-start | bytes 1572872 | tf_op jit(solution)/shard_map/ppermute | solution.py:24
  88.4 23.4 %copy-start.5 = (bf16[64,4096]{1,0:T(8,128)(2,1)S(1)}, bf16[64,4096]{1,0:T(8,128)(2,1)}, u32[]{:S(2)}) copy-start(bf16[64,4096]{1,0:T(8,128)(2,1)} %copy-done.4) | copy-start | bytes 1572868
  88.5 4.5 %collective-permute-start.3 = (bf16[96,256]{1,0:T(8,128)(2,1)S(1)}, bf16[96,256]{1,0:T(8,128)(2,1)S(1)}, u32[]{:S(2)}, u32[]{:S(2)}) collective-permute-start(bf16[96,256]{1,0:T(8,128)(2,1)S(1)} %get-tuple-element.40), channel_id=1, source_target_pairs={{0,16},{16,0},{1,17},{17,1},{2,18},{18,2},{3,19},{19,3},{4,20},{20... | collective-permute-start | bytes 147464 | tf_op jit(solution)/shard_map/ppermute | solution.py:24
  106.1 5.7 %collective-permute-start.4 = (bf16[8,2,96,256]{3,2,1,0:T(8,128)(2,1)S(1)}, bf16[8,2,96,256]{3,2,1,0:T(8,128)(2,1)S(1)}, u32[]{:S(2)}, u32[]{:S(2)}) collective-permute-start(bf16[8,2,96,256]{3,2,1,0:T(8,128)(2,1)S(1)} %all_to_all.31.refs_4_), channel_id=1, source_target_pairs={{0,1},{1,0},{2,3},{3,2},{4,5},{5,4},{6,7},{7,6},{8,9},{9,8},{10,11... | collective-permute-start | bytes 2359304 | tf_op jit(solution)/shard_map/ppermute | solution.py:24
  122.6 26.1 %copy-start.3 = (f32[256,256]{1,0:T(8,128)S(1)}, f32[256,256]{1,0:T(8,128)}, u32[]{:S(2)}) copy-start(f32[256,256]{1,0:T(8,128)} %cols_ref.1) | copy-start | bytes 786436
  163.8 3.8 %collective-permute-start.5 = (bf16[8,12,16,256]{3,2,1,0:T(8,128)(2,1)S(1)}, bf16[8,12,16,256]{3,2,1,0:T(8,128)(2,1)S(1)}, u32[]{:S(2)}, u32[]{:S(2)}) collective-permute-start(bf16[8,12,16,256]{3,2,1,0:T(8,128)(2,1)S(1)} %all_to_all.33.near_ref), channel_id=1, source_target_pairs={{0,1},{1,0},{2,3},{3,2},{4,5},{5,4},{6,7},{7,6},{8,9},{9,8},{10,11... | collective-permute-start | bytes 2359304 | tf_op jit(solution)/shard_map/ppermute | solution.py:24

commit v2 on v1

--- a/solution.py
+++ b/solution.py
@@ -123,7 +123,7 @@
     nv = pot.shape[0]
     half = slots // 2
     outs = [jax.ShapeDtypeStruct((half // group, nv, group * rows), F32)]
-    outs += [jax.ShapeDtypeStruct(occ.shape, occ.dtype)] * (2 * (1 - part))
+    outs += [jax.ShapeDtypeStruct(occ.shape, occ.dtype)] * (3 * (1 - part))
     return pl.pallas_call(
         functools.partial(project_kernel, start=part * half, group=group),
         in_specs=[WHOLE] * 3,
@@ -137,57 +137,57 @@
     )(occ, basis, pot)
 
 
-def respond_kernel(*refs, group):
-    *occ_refs, basis_ref, far_ref, near_ref, out_ref = refs
-    blocks, _, nv, _ = far_ref.shape
-    owners, size, side = out_ref.shape
-    per_owner = nv // owners
+def respond_kernel(*refs, first, group):
+    own_occ, other_occ, basis_ref, guess_ref, *sums, out_ref = refs
+    blocks, _, nv, _ = guess_ref.shape
+    lines, _, side = own_occ.shape
     per_step = 8
 
     def step(t, carry):
-        lines = []
+        totals = []
         for r in range(per_step):
             k = t * per_step + r
             cut = pl.ds(pl.multiple_of(k * side, side), side)
             parts = halves(basis_ref, cut)
-            total = None
-            for p, occ_ref in enumerate(occ_refs):
+            total = sums[0][k] if sums else None
+            for p, occ_ref in enumerate((own_occ, other_occ)):
                 occ = occ_ref[k]
-                for h, ref in enumerate((far_ref, near_ref)):
-                    for b in range(blocks):
-                        base = (h * blocks + b) * group
-                        places = range(base, base + group)
-                        pairs = products(occ, places, parts[:: 1 - 2 * p])
-                        term = jnp.dot(ref[b, p], pairs, preferred_element_type=F32)
-                        total = term if total is None else total + term
-            lines.append(total)
-        rows = per_step * per_owner
-        for n in range(owners):
-            piece = [line[n * per_owner : (n + 1) * per_owner] for line in lines]
-            piece = jnp.concatenate(piece, axis=0).astype(out_ref.dtype)
-            out_ref[n, pl.ds(pl.multiple_of(t * rows, rows), rows), :] = piece
+                for b in range(blocks):
+                    places = range(first + b * group, first + (b + 1) * group)
+                    pairs = products(occ, places, parts[:: 1 - 2 * p])
+                    term = jnp.dot(guess_ref[b, p], pairs, preferred_element_type=F32)
+                    total = term if total is None else total + term
+            if not sums:
+                out_ref[k] = total
+            totals.append(total)
+        if sums:
+            owners = out_ref.shape[0]
+            per_owner = nv // owners
+            rows = per_step * per_owner
+            for n in range(owners):
+                piece = [total[n * per_owner : (n + 1) * per_owner] for total in totals]
+                piece = jnp.concatenate(piece, axis=0).astype(out_ref.dtype)
+                out_ref[n, pl.ds(pl.multiple_of(t * rows, rows), rows), :] = piece
         return carry
 
-    lax.fori_loop(0, size // per_owner // per_step, step, 0)
-
-
-def respond(occs, basis, far, near, group, owners):
-    lines, slots, _ = occs[0].shape
+    lax.fori_loop(0, lines // per_step, step, 0)
+
+
+def respond(occs, basis, guess, first, out, group, *sums):
+    _, slots, _ = occs[0].shape
     rows, points = basis.shape
-    nv = far.shape[2]
+    nv = guess.shape[2]
     return pl.pallas_call(
-        functools.partial(respond_kernel, group=group),
-        in_specs=[WHOLE] * (len(occs) + 3),
+        functools.partial(respond_kernel, first=first, group=group),
+        in_specs=[WHOLE] * (4 + len(sums)),
         out_specs=WHOLE,
-        out_shape=jax.ShapeDtypeStruct((owners, lines * nv // owners, SIDE), BF16),
+        out_shape=out,
         cost_estimate=pl.CostEstimate(
-            flops=2 * len(occs) * slots * rows * points * nv,
-            bytes_accessed=6_000_000,
-            transcendentals=0,
+            flops=2 * slots * rows * points * nv, bytes_accessed=4_000_000, transcendentals=0
         ),
         compiler_params=ROOM,
         name="respond",
-    )(*occs, basis, far, near)
+    )(*occs, basis, guess, *sums)
 
 
 def columns_kernel(parts_ref, cols_ref, out_ref):
@@ -286,7 +286,7 @@
         for c in (core, 1 - core)
     ]
     out = jax.ShapeDtypeStruct((nx * mine, points), BF16)
-    bases = small_call(stack_kernel, [out] * 3, orbitals, partner)
+    bases = small_call(stack_kernel, [out] * 4, orbitals, partner)
     early = (occ, bases, pot, weight, mixes)
     occ, bases, pot, weight, mixes = lax.optimization_barrier(early)
 
@@ -303,7 +303,10 @@
     guesses = jnp.stack([kept, swapped(given, XH)])
     near_guess = exchanged(jnp.broadcast_to(guesses, (chips, *guesses.shape)), CHIP)
     far_guess = swapped(near_guess, CORE)
-    response = respond((occs[1], other_occ), bases[2], far_guess, near_guess, group, nz)
+    out = jax.ShapeDtypeStruct((lines, nv // nx, SIDE), F32)
+    part = respond((occs[1], other_occ), bases[2], near_guess, half, out, group)
+    out = jax.ShapeDtypeStruct((nz, lines * per_owner, SIDE), BF16)
+    response = respond((occs[2], other_occ), bases[3], far_guess, 0, out, group, part)
 
     out = jax.ShapeDtypeStruct((chips, per_owner, lines, SIDE), BF16)
     columns = small_call(columns_kernel, out, exchanged(response, Z), coul_cols)

time: 169 us -> 168 us (level)
  waiting for transfers between devices: 35.2 us -> 32.4 us
    ppermute x6, waiting for transfers between devices: 17.4 us -> 15.5 us  [swapped(): return lax.ppermute(shard, axis, SWAP)]
    pallas_call x1 -> x2, Pallas kernels: 10.8 us -> 11.1 us  [respond(): pl.pallas_call(functools.partial(respond_kernel, first=first, group=group...]
  transfers between devices with their start and end apart: 8 -> 8, of which waited for: 6 -> 5; matrix products, arithmetic and copies ran while one was open for 2% -> 2% of each run, Pallas kernels for 4% -> 8%
where the time goes in v2:
time: 168 us; the launch traced here: 167 us
  blocking collectives  69.6 us (41%)
  waiting for transfers between devices  32.4 us (19%)
  starting transfers between devices  30.2 us (18%)
  Pallas kernels  28.3 us (17%)
  local copies, waits for them, and re-layouts  4.85 us (3%)
    all_to_all x4, blocking collectives, exchanged(): return lax.all_to_all(parts, axes, split_axis=0, concat_axis=0, tiled=True)  69.6 us
    all_to_all x2, waiting for transfers between devices, exchanged(): return lax.all_to_all(parts, axes, split_axis=0, concat_axis=0, tiled=True)  17 us
    all_to_all x2, starting transfers between devices, exchanged(): return lax.all_to_all(parts, axes, split_axis=0, concat_axis=0, tiled=True)  16 us
    ppermute x6, waiting for transfers between devices, swapped(): return lax.ppermute(shard, axis, SWAP)  15.5 us
    ppermute x6, starting transfers between devices, swapped(): return lax.ppermute(shard, axis, SWAP)  14.3 us
    pallas_call x2, Pallas kernels, respond(): pl.pallas_call(functools.partial(respond_kernel, first=first, group=group...  11.1 us
    pallas_call x2, Pallas kernels, project(): pl.pallas_call(functools.partial(project_kernel, start=part * half, group...  10.8 us
    pallas_call x6, Pallas kernels, small_call(): return pl.pallas_call(kernel, out_shape=out, compiler_params=ROOM)(*args)  4.61 us
  transfers between devices with their start and end apart: 8, of which 5 were waited for; matrix products, arithmetic and copies ran while one was open for 2% of the time, Pallas kernels for 8%

profile of v2, /device:TPU:1, one launch (start us, length us, event | category | flops | bytes accessed | tf_op | source)
XLA Modules:
  0.0 167.2 jit_solution(14357904518016995690)
XLA Ops:
  0.0 1.7 %split.1 = bf16[16,32,256]{2,1,0:T(8,128)(2,1)} custom-call(bf16[32,4096]{1,0:T(8,128)(2,1)} %first_ref.1), custom_call_target="tpu_custom_call" | custom-call | tf_op jit(solution)/shard_map/split/pallas_call | solution.py:45
  1.8 11.7 %all-to-all-start = ((bf16[16,32,256]{2,1,0:T(8,128)(2,1)}), bf16[16,32,256]{2,1,0:T(8,128)(2,1)S(1)}, u32[]{:S(2)}, u32[]{:S(2)}) async-start(bf16[16,32,256]{2,1,0:T(8,128)(2,1)} %split.1), calls=%async_computation | async-start | bytes 524288 | tf_op jit(solution)/shard_map/all_to_all | solution.py:28
  13.5 2.9 %collective-permute-start = (bf16[32,4096]{1,0:T(8,128)(2,1)}, bf16[32,4096]{1,0:T(8,128)(2,1)}, u32[]{:S(2)}, u32[]{:S(2)}) collective-permute-start(bf16[32,4096]{1,0:T(8,128)(2,1)} %first_ref.1), channel_id=1, source_target_pairs={{0,16},{16,0},{1,17},{17,1},{2,18},{18,2},{3,19},{19,3},{4,20},{20... | collective-permute-start | bytes 786440 | tf_op jit(solution)/shard_map/ppermute | solution.py:24
  16.4 0.9 fusion.19
  17.4 0.8 fusion
  18.2 7.4 %all-to-all-done = bf16[16,32,256]{2,1,0:T(8,128)(2,1)S(1)} async-done(((bf16[16,32,256]{2,1,0:T(8,128)(2,1)}), bf16[16,32,256]{2,1,0:T(8,128)(2,1)S(1)}, u32[]{:S(2)}, u32[]{:S(2)}) %all-to-all-start) | async-done | bytes 262176 | tf_op jit(solution)/shard_map/all_to_all | solution.py:28
  25.6 1.1 shard_map.64
  26.6 4.2 %all-to-all-start.1 = ((bf16[16,64,256]{2,1,0:T(8,128)(2,1)}), bf16[16,64,256]{2,1,0:T(8,128)(2,1)}, u32[]{:S(2)}, u32[]{:S(2)}) async-start(bf16[16,64,256]{2,1,0:T(8,128)(2,1)} %shard_map.64), calls=%async_computation.1 | async-start | bytes 1048576 | tf_op jit(solution)/shard_map/all_to_all | solution.py:28
  31.8 0.4 dynamic-slice_reduce_fusion
  32.6 0.6 shard_map.66.pot_ref
  33.5 1.1 shard_map.65
  34.6 0.8 copy-done.4
  35.4 0.8 copy-done.6
  36.2 0.8 copy-done.8
  37.0 9.6 %all-to-all-done.1.occ_ref = bf16[16,64,256]{2,1,0:T(8,128)(2,1)} async-done(((bf16[16,64,256]{2,1,0:T(8,128)(2,1)}), bf16[16,64,256]{2,1,0:T(8,128)(2,1)}, u32[]{:S(2)}, u32[]{:S(2)}) %all-to-all-start.1) | async-done | bytes 524320 | tf_op jit(solution)/shard_map/all_to_all | solution.py:28
  46.6 6.0 %project.2 = (f32[8,192,256]{2,1,0:T(8,128)S(1)}, bf16[16,64,256]{2,1,0:T(8,128)(2,1)S(1)}, bf16[16,64,256]{2,1,0:T(8,128)(2,1)S(1)}, bf16[16,64,256]{2,1,0:T(8,128)(2,1)S(1)}) custom-call(bf16[16,64,256]{2,1,0:T(8,128)(2,1)} %all-to-all-done.1.occ_ref, bf16[64,4096]{1,0:T(8,128)(2,1)S(1)} %get-tuple-element.29.basis_ref, ...), custom_call_target="tpu_custom_call" | custom-call | flops 3221225472 | bytes 4000000 | tf_op jit(solution)/shard_map/project/pallas_call | solution.py:127
  52.6 4.7 %collective-permute-start.2 = (f32[8,192,256]{2,1,0:T(8,128)S(1)}, f32[8,192,256]{2,1,0:T(8,128)S(1)}, u32[]{:S(2)}, u32[]{:S(2)}) collective-permute-start(f32[8,192,256]{2,1,0:T(8,128)S(1)} %get-tuple-element.37), channel_id=1, source_target_pairs={{0,1},{1,0},{2,3},{3,2},{4,5},{5,4},{6,7},{7,6},{8,9},{9,8},{10,11... | collective-permute-start | bytes 4718600 | tf_op jit(solution)/shard_map/ppermute | solution.py:24
  57.7 4.8 %project.3.near_ref = f32[8,192,256]{2,1,0:T(8,128)S(1)} custom-call(bf16[16,64,256]{2,1,0:T(8,128)(2,1)S(1)} %get-tuple-element.32.occ_ref, bf16[64,4096]{1,0:T(8,128)(2,1)S(1)} %copy-done.9, bf16[192,4096]{1,0:T(8,128)(2,1)S(1)} %shard_map.66.pot_ref), custom_call_target="tpu_custom_call" | custom-call | flops 3221225472 | bytes 4000000 | tf_op jit(solution)/shard_map/project/pallas_call | solution.py:127
  62.5 10.0 %collective-permute-done.1.refs_1_ = bf16[16,64,256]{2,1,0:T(8,128)(2,1)S(1)} collective-permute-done((bf16[16,64,256]{2,1,0:T(8,128)(2,1)}, bf16[16,64,256]{2,1,0:T(8,128)(2,1)S(1)}, u32[]{:S(2)}, u32[]{:S(2)}) %collective-permute-start.1) | collective-permute-done | bytes 524320 | tf_op jit(solution)/shard_map/ppermute | solution.py:24
  72.6 15.8 %all_to_all.30 = bf16[8,192,256]{2,1,0:T(8,128)(2,1)S(1)} all-to-all(bf16[8,192,256]{2,1,0:T(8,128)(2,1)S(1)} %shard_map.67), channel_id=1, replica_groups=mesh['z'=8,'x_hi'=2,'y'=4,'x_lo'=2,'core'=2] {'y','x_lo'}, dimensions={0} | all-to-all | bytes 1572864 | tf_op jit(solution)/shard_map/all_to_all | solution.py:28
  88.5 1.0 collective-permute-start.3
  89.5 3.6 %collective-permute-done.3 = bf16[96,256]{1,0:T(8,128)(2,1)S(1)} collective-permute-done((bf16[96,256]{1,0:T(8,128)(2,1)S(1)}, bf16[96,256]{1,0:T(8,128)(2,1)S(1)}, u32[]{:S(2)}, u32[]{:S(2)}) %collective-permute-start.3) | collective-permute-done | bytes 49184 | tf_op jit(solution)/shard_map/ppermute | solution.py:24
  93.2 13.0 %all_to_all.31.refs_3_ = bf16[8,2,96,256]{3,2,1,0:T(8,128)(2,1)S(1)} all-to-all(bf16[8,2,96,256]{3,2,1,0:T(8,128)(2,1)S(1)} %broadcast_in_dim.30), channel_id=1, replica_groups=mesh['z'=8,'x_hi'=2,'y'=4,'x_lo'=2,'core'=2] {'y','x_lo'}, dimensions={0} | all-to-all | bytes 1572864 | tf_op jit(solution)/shard_map/all_to_all | solution.py:28
  106.2 3.7 %collective-permute-start.4 = (bf16[8,2,96,256]{3,2,1,0:T(8,128)(2,1)S(1)}, bf16[8,2,96,256]{3,2,1,0:T(8,128)(2,1)S(1)}, u32[]{:S(2)}, u32[]{:S(2)}) collective-permute-start(bf16[8,2,96,256]{3,2,1,0:T(8,128)(2,1)S(1)} %all_to_all.31.refs_3_), channel_id=1, source_target_pairs={{0,1},{1,0},{2,3},{3,2},{4,5},{5,4},{6,7},{7,6},{8,9},{9,8},{10,11... | collective-permute-start | bytes 2359304 | tf_op jit(solution)/shard_map/ppermute | solution.py:24
  109.9 5.5 %respond.2.refs_4_ = f32[16,96,256]{2,1,0:T(8,128)S(1)} custom-call(bf16[16,64,256]{2,1,0:T(8,128)(2,1)S(1)} %get-tuple-element.39.refs_0_, bf16[16,64,256]{2,1,0:T(8,128)(2,1)S(1)} %collective-permute-done.1.refs_1_, bf16[64,4096]{1,0:T(8,128)(2,1)S(1)} %copy-done.7, bf16[8,2,96,256]{3,2,1,0:T(8,128)(2,1)S(1)} %all_to_all.31.refs_3_), custom_call_target="tpu_custom_call" | custom-call | flops 3221225472 | bytes 4000000 | tf_op jit(solution)/shard_map/respond/pallas_call | solution.py:180
  115.5 5.6 %respond.3 = bf16[8,192,256]{2,1,0:T(8,128)(2,1)S(1)} custom-call(bf16[16,64,256]{2,1,0:T(8,128)(2,1)S(1)} %get-tuple-element.31.refs_0_, bf16[16,64,256]{2,1,0:T(8,128)(2,1)S(1)} %collective-permute-done.1.refs_1_, bf16[64,4096]{1,0:T(8,128)(2,1)S(1)} %copy-done.5, bf16[8,2,96,256]{3,2,1,0:T(8,128)(2,1)S(1)} %collective-permute-done.4.refs_3_, ...), custom_call_target="tpu_custom_call" | custom-call | flops 3221225472 | bytes 4000000 | tf_op jit(solution)/shard_map/respond/pallas_call | solution.py:180
  121.1 26.2 %all_to_all.32.parts_ref = bf16[8,192,256]{2,1,0:T(8,128)(2,1)S(1)} all-to-all(bf16[8,192,256]{2,1,0:T(8,128)(2,1)S(1)} %respond.3), channel_id=1, replica_groups=mesh['z'=8,'x_hi'=2,'y'=4,'x_lo'=2,'core'=2] {'z'}, dimensions={0} | all-to-all | bytes 1572864 | tf_op jit(solution)/shard_map/all_to_all | solution.py:28
  147.3 0.7 shard_map.68
  148.0 14.6 %all_to_all.33.near_ref = bf16[8,12,16,256]{3,2,1,0:T(8,128)(2,1)S(1)} all-to-all(bf16[8,12,16,256]{3,2,1,0:T(8,128)(2,1)S(1)} %shard_map.68), channel_id=1, replica_groups=mesh['z'=8,'x_hi'=2,'y'=4,'x_lo'=2,'core'=2] {'y','x_lo'}, dimensions={0} | all-to-all | bytes 1572864 | tf_op jit(solution)/shard_map/all_to_all | solution.py:28
  162.6 1.7 %collective-permute-start.5 = (bf16[8,12,16,256]{3,2,1,0:T(8,128)(2,1)S(1)}, bf16[8,12,16,256]{3,2,1,0:T(8,128)(2,1)S(1)}, u32[]{:S(2)}, u32[]{:S(2)}) collective-permute-start(bf16[8,12,16,256]{3,2,1,0:T(8,128)(2,1)S(1)} %all_to_all.33.near_ref), channel_id=1, source_target_pairs={{0,1},{1,0},{2,3},{3,2},{4,5},{5,4},{6,7},{7,6},{8,9},{9,8},{10,11... | collective-permute-start | bytes 2359304 | tf_op jit(solution)/shard_map/ppermute | solution.py:24
  164.2 1.9 %collective-permute-done.5.far_ref = bf16[8,12,16,256]{3,2,1,0:T(8,128)(2,1)S(1)} collective-permute-done((bf16[8,12,16,256]{3,2,1,0:T(8,128)(2,1)S(1)}, bf16[8,12,16,256]{3,2,1,0:T(8,128)(2,1)S(1)}, u32[]{:S(2)}, u32[]{:S(2)}) %collective-permute-start.5) | collective-permute-done | bytes 786464 | tf_op jit(solution)/shard_map/ppermute | solution.py:24
  166.1 1.0 shard_map.69
  (46 shorter events, 2.4 us)
Async XLA Ops:
  0.0 31.6 %copy-start = (f32[256,256]{1,0:T(8,128)S(1)}, f32[256,256]{1,0:T(8,128)}, u32[]{:S(2)}) copy-start(f32[256,256]{1,0:T(8,128)} %param.10) | copy-start | bytes 786436
  0.0 30.9 %copy-start.10 = (s32[128]{0:T(128)S(1)}, s32[128]{0:T(128)}, u32[]{:S(2)}) copy-start(s32[128]{0:T(128)} %param.9) | copy-start | bytes 1540
  0.0 31.0 %copy-start.11 = (f32[512]{0:T(512)S(1)}, f32[512]{0:T(512)}, u32[]{:S(2)}) copy-start(f32[512]{0:T(512)} %param.8) | copy-start | bytes 6148
  1.8 30.8 %copy-start.1 = (bf16[192,4096]{1,0:T(8,128)(2,1)S(1)}, bf16[192,4096]{1,0:T(8,128)(2,1)}, u32[]{:S(2)}) copy-start(bf16[192,4096]{1,0:T(8,128)(2,1)} %rows_ref.3) | copy-start | bytes 4718596
  1.8 23.8 %all-to-all-start = ((bf16[16,32,256]{2,1,0:T(8,128)(2,1)}), bf16[16,32,256]{2,1,0:T(8,128)(2,1)S(1)}, u32[]{:S(2)}, u32[]{:S(2)}) async-start(bf16[16,32,256]{2,1,0:T(8,128)(2,1)} %split.1), calls=%async_computation | async-start | bytes 524288 | tf_op jit(solution)/shard_map/all_to_all | solution.py:28
  13.5 19.7 %collective-permute-start = (bf16[32,4096]{1,0:T(8,128)(2,1)}, bf16[32,4096]{1,0:T(8,128)(2,1)}, u32[]{:S(2)}, u32[]{:S(2)}) collective-permute-start(bf16[32,4096]{1,0:T(8,128)(2,1)} %first_ref.1), channel_id=1, source_target_pairs={{0,16},{16,0},{1,17},{17,1},{2,18},{18,2},{3,19},{19,3},{4,20},{20... | collective-permute-start | bytes 786440 | tf_op jit(solution)/shard_map/ppermute | solution.py:24
  26.6 20.0 %all-to-all-start.1 = ((bf16[16,64,256]{2,1,0:T(8,128)(2,1)}), bf16[16,64,256]{2,1,0:T(8,128)(2,1)}, u32[]{:S(2)}, u32[]{:S(2)}) async-start(bf16[16,64,256]{2,1,0:T(8,128)(2,1)} %shard_map.64), calls=%async_computation.1 | async-start | bytes 1048576 | tf_op jit(solution)/shard_map/all_to_all | solution.py:28
  32.5 1.0 copy-start.2
  34.6 0.8 copy-start.4
  35.4 0.8 copy-start.6
  36.2 0.8 copy-start.8
  46.6 11.1 %copy-start.9 = (bf16[64,4096]{1,0:T(8,128)(2,1)S(1)}, bf16[64,4096]{1,0:T(8,128)(2,1)}, u32[]{:S(2)}) copy-start(bf16[64,4096]{1,0:T(8,128)(2,1)} %copy-done.8) | copy-start | bytes 1572868
  52.6 19.8 %collective-permute-start.2 = (f32[8,192,256]{2,1,0:T(8,128)S(1)}, f32[8,192,256]{2,1,0:T(8,128)S(1)}, u32[]{:S(2)}, u32[]{:S(2)}) collective-permute-start(f32[8,192,256]{2,1,0:T(8,128)S(1)} %get-tuple-element.37), channel_id=1, source_target_pairs={{0,1},{1,0},{2,3},{3,2},{4,5},{5,4},{6,7},{7,6},{8,9},{9,8},{10,11... | collective-permute-start | bytes 4718600 | tf_op jit(solution)/shard_map/ppermute | solution.py:24
  57.4 15.1 %collective-permute-start.1 = (bf16[16,64,256]{2,1,0:T(8,128)(2,1)}, bf16[16,64,256]{2,1,0:T(8,128)(2,1)S(1)}, u32[]{:S(2)}, u32[]{:S(2)}) collective-permute-start(bf16[16,64,256]{2,1,0:T(8,128)(2,1)} %all-to-all-done.1.occ_ref), channel_id=1, source_target_pairs={{0,16},{16,0},{1,17},{17,1},{2,18},{18,2},{3,19},{19,3},{4,20},{20... | collective-permute-start | bytes 1572872 | tf_op jit(solution)/shard_map/ppermute | solution.py:24
  88.5 21.5 %copy-start.7 = (bf16[64,4096]{1,0:T(8,128)(2,1)S(1)}, bf16[64,4096]{1,0:T(8,128)(2,1)}, u32[]{:S(2)}) copy-start(bf16[64,4096]{1,0:T(8,128)(2,1)} %copy-done.6) | copy-start | bytes 1572868
  88.5 4.5 %collective-permute-start.3 = (bf16[96,256]{1,0:T(8,128)(2,1)S(1)}, bf16[96,256]{1,0:T(8,128)(2,1)S(1)}, u32[]{:S(2)}, u32[]{:S(2)}) collective-permute-start(bf16[96,256]{1,0:T(8,128)(2,1)S(1)} %get-tuple-element.46), channel_id=1, source_target_pairs={{0,16},{16,0},{1,17},{17,1},{2,18},{18,2},{3,19},{19,3},{4,20},{20... | collective-permute-start | bytes 147464 | tf_op jit(solution)/shard_map/ppermute | solution.py:24
  106.2 9.3 %collective-permute-start.4 = (bf16[8,2,96,256]{3,2,1,0:T(8,128)(2,1)S(1)}, bf16[8,2,96,256]{3,2,1,0:T(8,128)(2,1)S(1)}, u32[]{:S(2)}, u32[]{:S(2)}) collective-permute-start(bf16[8,2,96,256]{3,2,1,0:T(8,128)(2,1)S(1)} %all_to_all.31.refs_3_), channel_id=1, source_target_pairs={{0,1},{1,0},{2,3},{3,2},{4,5},{5,4},{6,7},{7,6},{8,9},{9,8},{10,11... | collective-permute-start | bytes 2359304 | tf_op jit(solution)/shard_map/ppermute | solution.py:24
  109.9 5.5 %copy-start.5 = (bf16[64,4096]{1,0:T(8,128)(2,1)S(1)}, bf16[64,4096]{1,0:T(8,128)(2,1)}, u32[]{:S(2)}) copy-start(bf16[64,4096]{1,0:T(8,128)(2,1)} %copy-done.4) | copy-start | bytes 1572868
  121.1 26.2 %copy-start.3 = (f32[256,256]{1,0:T(8,128)S(1)}, f32[256,256]{1,0:T(8,128)}, u32[]{:S(2)}) copy-start(f32[256,256]{1,0:T(8,128)} %cols_ref.1) | copy-start | bytes 786436
  162.6 3.6 %collective-permute-start.5 = (bf16[8,12,16,256]{3,2,1,0:T(8,128)(2,1)S(1)}, bf16[8,12,16,256]{3,2,1,0:T(8,128)(2,1)S(1)}, u32[]{:S(2)}, u32[]{:S(2)}) collective-permute-start(bf16[8,12,16,256]{3,2,1,0:T(8,128)(2,1)S(1)} %all_to_all.33.near_ref), channel_id=1, source_target_pairs={{0,1},{1,0},{2,3},{3,2},{4,5},{5,4},{6,7},{7,6},{8,9},{9,8},{10,11... | collective-permute-start | bytes 2359304 | tf_op jit(solution)/shard_map/ppermute | solution.py:24

commit v3 on v2

--- a/solution.py
+++ b/solution.py
@@ -12,7 +12,8 @@
 Z, XH, Y, XL, CORE = "z", "x_hi", "y", "x_lo", "core"
 CELL = (Y, XL, CORE)
 ORB = (Z, XH)
-CHIP = (Y, XL)
+CHIP = (XL, Y)
+SWEEP = (XH, Z)
 F32, BF16 = jnp.float32, jnp.bfloat16
 HIGH = lax.Precision.HIGHEST
 SWAP = ((0, 1), (1, 0))
@@ -60,7 +61,7 @@
     picked = jnp.dot(chosen, rows_ref[...], preferred_element_type=F32).astype(BF16)
     slots = out_ref.shape[1]
     for k in range(out_ref.shape[0]):
-        n = k % (count // slots)
+        n = k * (count // slots) // out_ref.shape[0]
         out_ref[k] = picked[n * slots : (n + 1) * slots]
 
 
@@ -141,7 +142,7 @@
     own_occ, other_occ, basis_ref, guess_ref, *sums, out_ref = refs
     blocks, _, nv, _ = guess_ref.shape
     lines, _, side = own_occ.shape
-    per_step = 8
+    per_step = 16
 
     def step(t, carry):
         totals = []
@@ -240,7 +241,7 @@
     nz, nx, ny, nl, nc = (lax.axis_size(a) for a in (Z, XH, Y, XL, CORE))
     z, xh, y, xl, core = (lax.axis_index(a) for a in (Z, XH, Y, XL, CORE))
     chips = ny * nl
-    chip = y * nl + xl
+    chip = xl * ny + y
     width = points // (nz * nx)
     slots = nocc // nx
     half = slots // nc
@@ -250,16 +251,19 @@
     per_owner = nv // (nz * nx)
 
     partner = swapped(orbitals, XH)
-    by_points = exchanged(split(orbitals, nz * nx), ORB)
+    by_points = exchanged(split(orbitals, nz * nx), SWEEP)
 
     def part_of(values, start, count):
         return lax.dynamic_slice_in_dim(values, start, count)
 
     starts = [s * slots + c * half for s in range(nx) for c in (1 - core, core)]
-    wanted = jnp.concatenate([part_of(occ_index, s, half) for s in starts])[:, None]
+    wanted = jnp.concatenate([part_of(occ_index, s, half) for s in starts])
+    group_of = wanted // mine
+    wanted = (group_of % nx * nz + group_of // nx) * mine + wanted % mine
+    wanted = wanted[:, None]
     copies = jax.ShapeDtypeStruct((nz * nx, slots, width), BF16)
     spread = small_call(pick_kernel, copies, wanted, by_points.reshape(norb, width))
-    occ = exchanged(spread, ORB)
+    occ = exchanged(spread, SWEEP)
 
     place = jnp.arange(nv, dtype=jnp.int32)
     side = (xh + 1 + place // (nz * per_owner)) % nx
@@ -279,7 +283,8 @@
     weight = -2.0 * basis_empty[None, :] / (own_levels[:, None] + basis_levels[None, :])
     weight = (weight / volume).reshape(1, group * nx * mine)
 
-    my_rows = part_of(coul_rows, (chip * nc + core) * lines, lines)
+    my_rows = part_of(coul_rows, ((y * nl + xl) * nc + core) * lines, lines)
+    my_rows = jnp.swapaxes(my_rows.reshape(lines, ny, nl, nc, lines), 1, 2)
     my_rows = my_rows.reshape(lines, chips, nc, lines)
     mixes = [
         lax.dynamic_index_in_dim(my_rows, c, 2, keepdims=False).reshape(lines, chips * lines)

time: 168 us -> 166 us (0.988)
  waiting for transfers between devices: 32.4 us -> 29.8 us
    ppermute x6, starting transfers between devices: 14.3 us -> 16.2 us  [swapped(): return lax.ppermute(shard, axis, SWAP)]
    all_to_all x2, waiting for transfers between devices: 17 us -> 15.2 us  [exchanged(): return lax.all_to_all(parts, axes, split_axis=0, concat_axis=0, tiled=True)]
  transfers between devices with their start and end apart: 8 -> 8, of which waited for: 5 -> 5; matrix products, arithmetic and copies ran while one was open for 2% -> 2% of each run, Pallas kernels for 8% -> 9%
where the time goes in v3:
time: 166 us
  blocking collectives  69.7 us (42%)
  starting transfers between devices  30.9 us (19%)
  waiting for transfers between devices  29.8 us (18%)
  Pallas kernels  28 us (17%)
  local copies, waits for them, and re-layouts  5.23 us (3%)
    all_to_all x4, blocking collectives, exchanged(): return lax.all_to_all(parts, axes, split_axis=0, concat_axis=0, tiled=True)  69.7 us
    ppermute x6, starting transfers between devices, swapped(): return lax.ppermute(shard, axis, SWAP)  16.2 us
    all_to_all x2, waiting for transfers between devices, exchanged(): return lax.all_to_all(parts, axes, split_axis=0, concat_axis=0, tiled=True)  15.2 us
    all_to_all x2, starting transfers between devices, exchanged(): return lax.all_to_all(parts, axes, split_axis=0, concat_axis=0, tiled=True)  14.6 us
    ppermute x6, waiting for transfers between devices, swapped(): return lax.ppermute(shard, axis, SWAP)  14.6 us
    pallas_call x2, Pallas kernels, project(): pl.pallas_call(functools.partial(project_kernel, start=part * half, group...  10.8 us
    pallas_call x2, Pallas kernels, respond(): pl.pallas_call(functools.partial(respond_kernel, first=first, group=group...  10.8 us
    pallas_call x6, Pallas kernels, small_call(): return pl.pallas_call(kernel, out_shape=out, compiler_params=ROOM)(*args)  4.6 us
  transfers between devices with their start and end apart: 8, of which 5 were waited for; matrix products, arithmetic and copies ran while one was open for 2% of the time, Pallas kernels for 9%

profile of v3, /device:TPU:1, one launch (start us, length us, event | category | flops | bytes accessed | tf_op | source)
XLA Modules:
  0.0 165.5 jit_solution(406425392579878868)
XLA Ops:
  0.0 3.6 %collective-permute-start = (bf16[32,4096]{1,0:T(8,128)(2,1)}, bf16[32,4096]{1,0:T(8,128)(2,1)}, u32[]{:S(2)}, u32[]{:S(2)}) collective-permute-start(bf16[32,4096]{1,0:T(8,128)(2,1)} %first_ref.1), channel_id=1, source_target_pairs={{0,16},{16,0},{1,17},{17,1},{2,18},{18,2},{3,19},{19,3},{4,20},{20... | collective-permute-start | bytes 786440 | tf_op jit(solution)/shard_map/ppermute | solution.py:25
  3.6 1.7 %split.1 = bf16[16,32,256]{2,1,0:T(8,128)(2,1)} custom-call(bf16[32,4096]{1,0:T(8,128)(2,1)} %first_ref.1), custom_call_target="tpu_custom_call" | custom-call | tf_op jit(solution)/shard_map/split/pallas_call | solution.py:46
  5.3 8.3 %all-to-all-start = ((bf16[16,32,256]{2,1,0:T(8,128)(2,1)}), bf16[16,32,256]{2,1,0:T(8,128)(2,1)S(1)}, u32[]{:S(2)}, u32[]{:S(2)}) async-start(bf16[16,32,256]{2,1,0:T(8,128)(2,1)} %split.1), calls=%async_computation | async-start | bytes 524288 | tf_op jit(solution)/shard_map/all_to_all | solution.py:29
  13.6 0.8 fusion
  14.4 0.9 dynamic-slice_bitcast_fusion.3
  15.4 0.7 dynamic_slice.43
  16.4 6.7 %all-to-all-done = bf16[16,32,256]{2,1,0:T(8,128)(2,1)S(1)} async-done(((bf16[16,32,256]{2,1,0:T(8,128)(2,1)}), bf16[16,32,256]{2,1,0:T(8,128)(2,1)S(1)}, u32[]{:S(2)}, u32[]{:S(2)}) %all-to-all-start) | async-done | bytes 262176 | tf_op jit(solution)/shard_map/all_to_all | solution.py:29
  23.0 1.1 shard_map.64
  24.1 6.3 %all-to-all-start.1 = ((bf16[16,64,256]{2,1,0:T(8,128)(2,1)}), bf16[16,64,256]{2,1,0:T(8,128)(2,1)}, u32[]{:S(2)}, u32[]{:S(2)}) async-start(bf16[16,64,256]{2,1,0:T(8,128)(2,1)} %shard_map.64), calls=%async_computation.1 | async-start | bytes 1048576 | tf_op jit(solution)/shard_map/all_to_all | solution.py:29
  32.7 1.1 shard_map.65
  33.8 0.8 copy-done.4
  34.6 0.8 copy-done.6
  35.4 0.8 copy-done.8
  36.2 8.6 %all-to-all-done.1.occ_ref = bf16[16,64,256]{2,1,0:T(8,128)(2,1)} async-done(((bf16[16,64,256]{2,1,0:T(8,128)(2,1)}), bf16[16,64,256]{2,1,0:T(8,128)(2,1)}, u32[]{:S(2)}, u32[]{:S(2)}) %all-to-all-start.1) | async-done | bytes 524320 | tf_op jit(solution)/shard_map/all_to_all | solution.py:29
  44.7 6.0 %project.2 = (f32[8,192,256]{2,1,0:T(8,128)S(1)}, bf16[16,64,256]{2,1,0:T(8,128)(2,1)S(1)}, bf16[16,64,256]{2,1,0:T(8,128)(2,1)S(1)}, bf16[16,64,256]{2,1,0:T(8,128)(2,1)S(1)}) custom-call(bf16[16,64,256]{2,1,0:T(8,128)(2,1)} %all-to-all-done.1.occ_ref, bf16[64,4096]{1,0:T(8,128)(2,1)S(1)} %get-tuple-element.29.basis_ref, ...), custom_call_target="tpu_custom_call" | custom-call | flops 3221225472 | bytes 4000000 | tf_op jit(solution)/shard_map/project/pallas_call | solution.py:128
  50.7 3.6 %collective-permute-start.2 = (f32[8,192,256]{2,1,0:T(8,128)S(1)}, f32[8,192,256]{2,1,0:T(8,128)S(1)}, u32[]{:S(2)}, u32[]{:S(2)}) collective-permute-start(f32[8,192,256]{2,1,0:T(8,128)S(1)} %get-tuple-element.37), channel_id=1, source_target_pairs={{0,1},{1,0},{2,3},{3,2},{4,5},{5,4},{6,7},{7,6},{8,9},{9,8},{10,11... | collective-permute-start | bytes 4718600 | tf_op jit(solution)/shard_map/ppermute | solution.py:25
  54.3 0.7 collective-permute-start.1
  55.0 4.8 %project.3.near_ref = f32[8,192,256]{2,1,0:T(8,128)S(1)} custom-call(bf16[16,64,256]{2,1,0:T(8,128)(2,1)S(1)} %get-tuple-element.32.occ_ref, bf16[64,4096]{1,0:T(8,128)(2,1)S(1)} %copy-done.9, bf16[192,4096]{1,0:T(8,128)(2,1)S(1)} %shard_map.66.pot_ref), custom_call_target="tpu_custom_call" | custom-call | flops 3221225472 | bytes 4000000 | tf_op jit(solution)/shard_map/project/pallas_call | solution.py:128
  59.8 9.6 %collective-permute-done.1.refs_1_ = bf16[16,64,256]{2,1,0:T(8,128)(2,1)S(1)} collective-permute-done((bf16[16,64,256]{2,1,0:T(8,128)(2,1)}, bf16[16,64,256]{2,1,0:T(8,128)(2,1)S(1)}, u32[]{:S(2)}, u32[]{:S(2)}) %collective-permute-start.1) | collective-permute-done | bytes 524320 | tf_op jit(solution)/shard_map/ppermute | solution.py:25
  69.5 16.0 %all_to_all.30 = bf16[8,192,256]{2,1,0:T(8,128)(2,1)S(1)} all-to-all(bf16[8,192,256]{2,1,0:T(8,128)(2,1)S(1)} %shard_map.67), channel_id=1, replica_groups=mesh['z'=8,'x_hi'=2,'y'=4,'x_lo'=2,'core'=2] {'x_lo','y'}, dimensions={0} | all-to-all | bytes 1572864 | tf_op jit(solution)/shard_map/all_to_all | solution.py:29
  85.7 1.4 collective-permute-start.3
  87.1 3.1 %collective-permute-done.3 = bf16[96,256]{1,0:T(8,128)(2,1)S(1)} collective-permute-done((bf16[96,256]{1,0:T(8,128)(2,1)S(1)}, bf16[96,256]{1,0:T(8,128)(2,1)S(1)}, u32[]{:S(2)}, u32[]{:S(2)}) %collective-permute-start.3) | collective-permute-done | bytes 49184 | tf_op jit(solution)/shard_map/ppermute | solution.py:25
  90.3 12.1 %all_to_all.31.refs_3_ = bf16[8,2,96,256]{3,2,1,0:T(8,128)(2,1)S(1)} all-to-all(bf16[8,2,96,256]{3,2,1,0:T(8,128)(2,1)S(1)} %broadcast_in_dim.16), channel_id=1, replica_groups=mesh['z'=8,'x_hi'=2,'y'=4,'x_lo'=2,'core'=2] {'x_lo','y'}, dimensions={0} | all-to-all | bytes 1572864 | tf_op jit(solution)/shard_map/all_to_all | solution.py:29
  102.4 4.8 %collective-permute-start.4 = (bf16[8,2,96,256]{3,2,1,0:T(8,128)(2,1)S(1)}, bf16[8,2,96,256]{3,2,1,0:T(8,128)(2,1)S(1)}, u32[]{:S(2)}, u32[]{:S(2)}) collective-permute-start(bf16[8,2,96,256]{3,2,1,0:T(8,128)(2,1)S(1)} %all_to_all.31.refs_3_), channel_id=1, source_target_pairs={{0,1},{1,0},{2,3},{3,2},{4,5},{5,4},{6,7},{7,6},{8,9},{9,8},{10,11... | collective-permute-start | bytes 2359304 | tf_op jit(solution)/shard_map/ppermute | solution.py:25
  107.2 5.4 %respond.2.refs_4_ = f32[16,96,256]{2,1,0:T(8,128)S(1)} custom-call(bf16[16,64,256]{2,1,0:T(8,128)(2,1)S(1)} %get-tuple-element.39.refs_0_, bf16[16,64,256]{2,1,0:T(8,128)(2,1)S(1)} %collective-permute-done.1.refs_1_, bf16[64,4096]{1,0:T(8,128)(2,1)S(1)} %copy-done.7, bf16[8,2,96,256]{3,2,1,0:T(8,128)(2,1)S(1)} %all_to_all.31.refs_3_), custom_call_target="tpu_custom_call" | custom-call | flops 3221225472 | bytes 4000000 | tf_op jit(solution)/shard_map/respond/pallas_call | solution.py:181
  112.6 5.4 %respond.3 = bf16[8,192,256]{2,1,0:T(8,128)(2,1)S(1)} custom-call(bf16[16,64,256]{2,1,0:T(8,128)(2,1)S(1)} %get-tuple-element.31.refs_0_, bf16[16,64,256]{2,1,0:T(8,128)(2,1)S(1)} %collective-permute-done.1.refs_1_, bf16[64,4096]{1,0:T(8,128)(2,1)S(1)} %copy-done.5, bf16[8,2,96,256]{3,2,1,0:T(8,128)(2,1)S(1)} %collective-permute-done.4.refs_3_, ...), custom_call_target="tpu_custom_call" | custom-call | flops 3221225472 | bytes 4000000 | tf_op jit(solution)/shard_map/respond/pallas_call | solution.py:181
  118.0 27.6 %all_to_all.32.parts_ref = bf16[8,192,256]{2,1,0:T(8,128)(2,1)S(1)} all-to-all(bf16[8,192,256]{2,1,0:T(8,128)(2,1)S(1)} %respond.3), channel_id=1, replica_groups=mesh['z'=8,'x_hi'=2,'y'=4,'x_lo'=2,'core'=2] {'z'}, dimensions={0} | all-to-all | bytes 1572864 | tf_op jit(solution)/shard_map/all_to_all | solution.py:29
  145.7 0.7 shard_map.68
  146.3 14.0 %all_to_all.33.near_ref = bf16[8,12,16,256]{3,2,1,0:T(8,128)(2,1)S(1)} all-to-all(bf16[8,12,16,256]{3,2,1,0:T(8,128)(2,1)S(1)} %shard_map.68), channel_id=1, replica_groups=mesh['z'=8,'x_hi'=2,'y'=4,'x_lo'=2,'core'=2] {'x_lo','y'}, dimensions={0} | all-to-all | bytes 1572864 | tf_op jit(solution)/shard_map/all_to_all | solution.py:29
  160.4 2.2 %collective-permute-start.5 = (bf16[8,12,16,256]{3,2,1,0:T(8,128)(2,1)S(1)}, bf16[8,12,16,256]{3,2,1,0:T(8,128)(2,1)S(1)}, u32[]{:S(2)}, u32[]{:S(2)}) collective-permute-start(bf16[8,12,16,256]{3,2,1,0:T(8,128)(2,1)S(1)} %all_to_all.33.near_ref), channel_id=1, source_target_pairs={{0,1},{1,0},{2,3},{3,2},{4,5},{5,4},{6,7},{7,6},{8,9},{9,8},{10,11... | collective-permute-start | bytes 2359304 | tf_op jit(solution)/shard_map/ppermute | solution.py:25
  162.5 1.9 %collective-permute-done.5.far_ref = bf16[8,12,16,256]{3,2,1,0:T(8,128)(2,1)S(1)} collective-permute-done((bf16[8,12,16,256]{3,2,1,0:T(8,128)(2,1)S(1)}, bf16[8,12,16,256]{3,2,1,0:T(8,128)(2,1)S(1)}, u32[]{:S(2)}, u32[]{:S(2)}) %collective-permute-start.5) | collective-permute-done | bytes 786464 | tf_op jit(solution)/shard_map/ppermute | solution.py:25
  164.5 1.0 shard_map.69
  (48 shorter events, 2.8 us)
Async XLA Ops:
  0.0 30.9 %copy-start = (f32[256,256]{1,0:T(8,128)S(1)}, f32[256,256]{1,0:T(8,128)}, u32[]{:S(2)}) copy-start(f32[256,256]{1,0:T(8,128)} %param.10) | copy-start | bytes 786436
  0.0 30.4 %copy-start.10 = (f32[512]{0:T(512)S(1)}, f32[512]{0:T(512)}, u32[]{:S(2)}) copy-start(f32[512]{0:T(512)} %param.8) | copy-start | bytes 6148
  0.0 32.3 %collective-permute-start = (bf16[32,4096]{1,0:T(8,128)(2,1)}, bf16[32,4096]{1,0:T(8,128)(2,1)}, u32[]{:S(2)}, u32[]{:S(2)}) collective-permute-start(bf16[32,4096]{1,0:T(8,128)(2,1)} %first_ref.1), channel_id=1, source_target_pairs={{0,16},{16,0},{1,17},{17,1},{2,18},{18,2},{3,19},{19,3},{4,20},{20... | collective-permute-start | bytes 786440 | tf_op jit(solution)/shard_map/ppermute | solution.py:25
  5.3 17.7 %all-to-all-start = ((bf16[16,32,256]{2,1,0:T(8,128)(2,1)}), bf16[16,32,256]{2,1,0:T(8,128)(2,1)S(1)}, u32[]{:S(2)}, u32[]{:S(2)}) async-start(bf16[16,32,256]{2,1,0:T(8,128)(2,1)} %split.1), calls=%async_computation | async-start | bytes 524288 | tf_op jit(solution)/shard_map/all_to_all | solution.py:29
  23.0 8.7 %copy-start.1 = (bf16[192,4096]{1,0:T(8,128)(2,1)S(1)}, bf16[192,4096]{1,0:T(8,128)(2,1)}, u32[]{:S(2)}) copy-start(bf16[192,4096]{1,0:T(8,128)(2,1)} %rows_ref.3) | copy-start | bytes 4718596
  24.1 20.6 %all-to-all-start.1 = ((bf16[16,64,256]{2,1,0:T(8,128)(2,1)}), bf16[16,64,256]{2,1,0:T(8,128)(2,1)}, u32[]{:S(2)}, u32[]{:S(2)}) async-start(bf16[16,64,256]{2,1,0:T(8,128)(2,1)} %shard_map.64), calls=%async_computation.1 | async-start | bytes 1048576 | tf_op jit(solution)/shard_map/all_to_all | solution.py:29
  31.7 1.0 copy-start.2
  33.7 0.8 copy-start.4
  34.6 0.8 copy-start.6
  35.4 0.8 copy-start.8
  44.7 10.3 %copy-start.9 = (bf16[64,4096]{1,0:T(8,128)(2,1)S(1)}, bf16[64,4096]{1,0:T(8,128)(2,1)}, u32[]{:S(2)}) copy-start(bf16[64,4096]{1,0:T(8,128)(2,1)} %copy-done.8) | copy-start | bytes 1572868
  50.7 18.7 %collective-permute-start.2 = (f32[8,192,256]{2,1,0:T(8,128)S(1)}, f32[8,192,256]{2,1,0:T(8,128)S(1)}, u32[]{:S(2)}, u32[]{:S(2)}) collective-permute-start(f32[8,192,256]{2,1,0:T(8,128)S(1)} %get-tuple-element.37), channel_id=1, source_target_pairs={{0,1},{1,0},{2,3},{3,2},{4,5},{5,4},{6,7},{7,6},{8,9},{9,8},{10,11... | collective-permute-start | bytes 4718600 | tf_op jit(solution)/shard_map/ppermute | solution.py:25
  54.3 15.1 %collective-permute-start.1 = (bf16[16,64,256]{2,1,0:T(8,128)(2,1)}, bf16[16,64,256]{2,1,0:T(8,128)(2,1)S(1)}, u32[]{:S(2)}, u32[]{:S(2)}) collective-permute-start(bf16[16,64,256]{2,1,0:T(8,128)(2,1)} %all-to-all-done.1.occ_ref), channel_id=1, source_target_pairs={{0,16},{16,0},{1,17},{17,1},{2,18},{18,2},{3,19},{19,3},{4,20},{20... | collective-permute-start | bytes 1572872 | tf_op jit(solution)/shard_map/ppermute | solution.py:25
  85.6 21.6 %copy-start.7 = (bf16[64,4096]{1,0:T(8,128)(2,1)S(1)}, bf16[64,4096]{1,0:T(8,128)(2,1)}, u32[]{:S(2)}) copy-start(bf16[64,4096]{1,0:T(8,128)(2,1)} %copy-done.6) | copy-start | bytes 1572868
  85.7 4.5 %collective-permute-start.3 = (bf16[96,256]{1,0:T(8,128)(2,1)S(1)}, bf16[96,256]{1,0:T(8,128)(2,1)S(1)}, u32[]{:S(2)}, u32[]{:S(2)}) collective-permute-start(bf16[96,256]{1,0:T(8,128)(2,1)S(1)} %get-tuple-element.46), channel_id=1, source_target_pairs={{0,16},{16,0},{1,17},{17,1},{2,18},{18,2},{3,19},{19,3},{4,20},{20... | collective-permute-start | bytes 147464 | tf_op jit(solution)/shard_map/ppermute | solution.py:25
  102.4 10.2 %collective-permute-start.4 = (bf16[8,2,96,256]{3,2,1,0:T(8,128)(2,1)S(1)}, bf16[8,2,96,256]{3,2,1,0:T(8,128)(2,1)S(1)}, u32[]{:S(2)}, u32[]{:S(2)}) collective-permute-start(bf16[8,2,96,256]{3,2,1,0:T(8,128)(2,1)S(1)} %all_to_all.31.refs_3_), channel_id=1, source_target_pairs={{0,1},{1,0},{2,3},{3,2},{4,5},{5,4},{6,7},{7,6},{8,9},{9,8},{10,11... | collective-permute-start | bytes 2359304 | tf_op jit(solution)/shard_map/ppermute | solution.py:25
  107.2 5.4 %copy-start.5 = (bf16[64,4096]{1,0:T(8,128)(2,1)S(1)}, bf16[64,4096]{1,0:T(8,128)(2,1)}, u32[]{:S(2)}) copy-start(bf16[64,4096]{1,0:T(8,128)(2,1)} %copy-done.4) | copy-start | bytes 1572868
  118.0 27.6 %copy-start.3 = (f32[256,256]{1,0:T(8,128)S(1)}, f32[256,256]{1,0:T(8,128)}, u32[]{:S(2)}) copy-start(f32[256,256]{1,0:T(8,128)} %cols_ref.1) | copy-start | bytes 786436
  160.4 4.1 %collective-permute-start.5 = (bf16[8,12,16,256]{3,2,1,0:T(8,128)(2,1)S(1)}, bf16[8,12,16,256]{3,2,1,0:T(8,128)(2,1)S(1)}, u32[]{:S(2)}, u32[]{:S(2)}) collective-permute-start(bf16[8,12,16,256]{3,2,1,0:T(8,128)(2,1)S(1)} %all_to_all.33.near_ref), channel_id=1, source_target_pairs={{0,1},{1,0},{2,3},{3,2},{4,5},{5,4},{6,7},{7,6},{8,9},{9,8},{10,11... | collective-permute-start | bytes 2359304 | tf_op jit(solution)/shard_map/ppermute | solution.py:25
